TPU v7x, 256 devices: a whole 4x4x8 slice. The times are simulated.
256 devices in a mesh: ens: 4 (over z_lo, core), gx: 16 (over x, z_hi), gy: 4 (over y).
Axes of the slice: x: 4, y: 4, z: 8 (z_hi: 4, z_lo: 2; z = z_hi * 2 + z_lo), core: 2. Of those that a mesh axis runs over, the one named last changes fastest.
Arguments:
- members: bfloat16 [64, 75, 256, 512], P(('ens', 'gx'), None, None, 'gy'), may hold values from -0.75 to 0.75
- spread: bfloat16 [75, 75], replicated, as said below
- sea_mask: int32 [256, 512], P(('ens', 'gx'), 'gy'), may hold values 0 or 1
- innovations: float32 [75, 256, 512], P(None, ('ens', 'gx'), 'gy'), may hold values from -19 to 19
- obs_error: float32 [75, 256, 512], P(None, ('ens', 'gx'), 'gy'), may hold values from 0.3 to 3
- static_scale: float32 [75, 256, 512], P(None, ('ens', 'gx'), 'gy'), may hold values from 2 to 8
Outputs:
- increment: float32 [75, 256, 512], P(None, ('ens', 'gx'), 'gy')
- alpha_fields: bfloat16 [64, 75, 256, 512], P(('ens', 'gx'), None, None, 'gy')
Inputs may be any that keep to these rules, and one draw needn't show every extreme that they name: `spread`: symmetric and positive definite. `sea_mask`: 1 marks sea, 0 land.
All inputs are finite; a program needn't handle non-finite values. No bound on the sum of `sea_mask` on one device may be relied on, other than what follows from the above.
Results may differ from a plain program's by a relative error of at most 0.0065.
Values may be sent and summed in bfloat16 or wider, within the bound.
No kernel may reach another device: no remote copies, remote signals or barrier semaphores. Data moves between devices by JAX's collectives and lax.ppermute only.
A program may use at most 128 MiB of HBM per device.

v0:
```python
import jax
import jax.numpy as jnp
from jax import lax
from jax.sharding import Mesh
from jax.sharding import PartitionSpec as P

GRIDS = 3
SWEEPS = 2
COARSE_SWEEPS = 4
ITERATIONS = 3
ENS_GX_GY = ("ens_0", "ens_1", "gx_0", "gx_1", "gy")
ENS_GX = ("ens_0", "ens_1", "gx_0", "gx_1")
diffusivity = 16.0
damping = 0.8


def padded_2(x, sides, width):
    edges = {}
    for axis, dim in sides:
        size, length = (lax.axis_size(axis), x.shape[dim])
        up = [(i, (i + 1) % size) for i in range(size - 1)]
        last = lax.slice_in_dim(x, length - width, length, axis=dim)
        leading = lax.slice_in_dim(x, 0, width, axis=dim)
        edges[dim] = (
            lax.ppermute(last, axis, up),
            lax.ppermute(leading, axis, [(b, a) for a, b in up]),
        )
    done = []
    for _, dim in sides:
        low, high = edges[dim]
        around = [(width, width) if d in done else (0, 0) for d in range(x.ndim)]
        x = jnp.concatenate([jnp.pad(low, around), x, jnp.pad(high, around)], axis=dim)
        done.append(dim)
    return x


def by_axis(x, axes):
    for axis in axes:
        x = lax.psum(x, axis)
    return x


def neighbours(padded):
    return padded[:, 2:, 1:-1] + padded[:, :-2, 1:-1] + padded[:, 1:-1, 2:] + padded[:, 1:-1, :-2]


def apply_level(values, strength, padded):
    return values + strength * (4.0 * values - neighbours(padded))


def relax(values, source, strength, padded):
    return values + damping * (source - apply_level(values, strength, padded)) / (
        1.0 + 4.0 * strength
    )


def framed(values):
    return padded_2(values.astype(jnp.bfloat16), ((ENS_GX, 1), ("gy", 2)), 1).astype(values.dtype)


def restrict(values):
    layer_count, row_count, column_count = values.shape
    return 0.25 * values.reshape(layer_count, row_count // 2, 2, column_count // 2, 2).sum(
        axis=(2, 4)
    )


def prolong(values):
    layer_count, row_count, column_count = values.shape
    spread_out = jnp.broadcast_to(
        values[:, :, None, :, None], (layer_count, row_count, 2, column_count, 2)
    )
    return spread_out.reshape(layer_count, 2 * row_count, 2 * column_count)


def coarse_solve(source, strength):
    factor = damping / (1.0 + 4.0 * strength)
    solution = factor * source
    for sweep_index in range(COARSE_SWEEPS - 1):
        padded = padded_2(solution, ((ENS_GX, 1), ("gy", 2)), 1)
        solution = relax(solution, source, strength, padded)
    return solution


def vcycle(source, grid_level):
    strength = diffusivity / 4.0**grid_level
    if grid_level == GRIDS - 1:
        return coarse_solve(source, strength)
    solution = damping / (1.0 + 4.0 * strength) * source
    solution = relax(solution, source, strength, framed(solution))
    remainder = source - apply_level(solution, strength, framed(solution))
    solution = solution + prolong(vcycle(restrict(remainder), grid_level + 1))
    for sweep_index in range(SWEEPS):
        solution = relax(solution, source, strength, framed(solution))
    return solution


def member_products(tiles, spread, masked):
    member_count, layer_count, row_count, column_count = tiles.shape
    product = (tiles * masked).astype(jnp.bfloat16)
    flat = product.reshape(member_count, layer_count, row_count * column_count)
    mixed = jnp.einsum("ij,kjc->kic", spread, flat, preferred_element_type=jnp.float32)
    return mixed.reshape(tiles.shape)


def local(members, spread, sea_mask, innovations, obs_error, static_scale):
    tiles = lax.all_to_all(members, ENS_GX, split_axis=2, concat_axis=0, tiled=True)
    sea = sea_mask.astype(jnp.float32)[None]

    def covariance(direction):
        masked = sea * direction
        mixed = member_products(tiles, spread, masked)
        ensemble = jnp.sum(tiles * mixed, axis=0)
        static = static_scale * vcycle(static_scale * masked, 0)
        return sea * (ensemble + static)

    def system(direction):
        cov_dir = covariance(direction)
        return (cov_dir, cov_dir + obs_error * direction)

    def merged(residual, image):
        return (
            by_axis(jnp.sum(residual * residual), ENS_GX_GY),
            by_axis(jnp.sum(residual * image), ENS_GX_GY),
        )

    weights = jnp.zeros_like(innovations)
    increment = jnp.zeros_like(innovations)
    residual = innovations
    cov_res, image_res = system(residual)
    norm_now, product = merged(residual, image_res)
    alpha = norm_now / product
    direction, along, cov_dir = (residual, image_res, cov_res)
    for iteration in range(ITERATIONS):
        weights = weights + alpha * direction
        increment = increment + alpha * cov_dir
        residual = residual - alpha * along
        if iteration + 1 < ITERATIONS:
            cov_res, image_res = system(residual)
            norm_next, product = merged(residual, image_res)
            ratio = norm_next / norm_now
            alpha = norm_next / (product - ratio * norm_next / alpha)
            direction = residual + ratio * direction
            along = image_res + ratio * along
            cov_dir = cov_res + ratio * cov_dir
            norm_now = norm_next
    final = member_products(tiles, spread, sea * weights).astype(jnp.bfloat16)
    alpha_fields = lax.all_to_all(final, ENS_GX, split_axis=0, concat_axis=2, tiled=True)
    return (increment, alpha_fields)


def solution(mesh):
    split = Mesh(
        mesh.devices.reshape(2, 2, 4, 4, mesh.shape["gy"]), ("ens_0", "ens_1", "gx_0", "gx_1", "gy")
    )
    return jax.shard_map(
        local,
        mesh=split,
        in_specs=(
            P(ENS_GX, None, None, "gy"),
            P(),
            P(ENS_GX, "gy"),
            P(None, ENS_GX, "gy"),
            P(None, ENS_GX, "gy"),
            P(None, ENS_GX, "gy"),
        ),
        out_specs=(P(None, ENS_GX, "gy"), P(ENS_GX, None, None, "gy")),
        check_vma=False,
    )
```

profile of v0, /device:TPU:8, one launch (start us, length us, event | category | flops | bytes accessed | tf_op | source)
XLA Modules:
  0.0 1073.8 jit_solution(13558479619360328652)
XLA Ops:
  0.6 7.9 copy.72
  8.5 12.3 %all-to-all-start = ((bf16[1,75,256,128]{3,1,0,2:T(8,128)(2,1)}), bf16[1,75,256,128]{3,1,0,2:T(8,128)(2,1)}, u32[]{:S(2)}, u32[]{:S(2)}) async-start(bf16[1,75,256,128]{3,1,0,2:T(8,128)(2,1)} %copy.72), calls=%async_computation | async-start | bytes 10485760 | tf_op jit(solution)/shard_map/all_to_all | solution.py:107
  22.6 5.4 collective-permute-start.1
  36.0 101.8 %collective-permute-done.2 = bf16[75,1,128]{0,2,1:T(8,128)(2,1)S(1)} collective-permute-done((bf16[75,1,128]{0,2,1:T(8,128)(2,1)S(1)}, bf16[75,1,128]{0,2,1:T(8,128)(2,1)S(1)}, u32[]{:S(2)}, u32[]{:S(2)}) %collective-permute-start.2) | collective-permute-done | bytes 19232 | tf_op jit(solution)/shard_map/ppermute | solution.py:26
  139.3 6.0 collective-permute-start.5
  155.1 6.7 collective-permute-start.9
  170.6 6.7 collective-permute-start.13
  186.1 6.7 collective-permute-start.17
  203.5 6.7 collective-permute-start.21
  220.9 6.7 collective-permute-start.25
  236.3 6.7 collective-permute-start.29
  253.8 6.7 collective-permute-start.33
  269.4 6.7 collective-permute-start.37
  291.7 7.7 collective-permute-start.41
  301.7 8.8 copy.131
  310.5 12.5 %reshape.178 = f32[64,75,512]{2,0,1:T(8,128)} reshape(f32[64,1,75,4,128]{4,3,0,2,1:T(4,128)} %bitcast.87) | data formatting | bytes 19660800 | tf_op jit(solution)/shard_map/convert_element_type | solution.py:113
  323.0 5.6 multiply_convert_fusion.3
  329.6 9.0 fusion.2
  341.1 22.0 %all-reduce.80 = (f32[]{:T(128)}, f32[]{:T(128)}) all-reduce(f32[]{:T(128)} %multiply_reduce_fusion.5, f32[]{:T(128)} %get-tuple-element.71), channel_id=1, replica_groups=mesh['ens_0'=2,'ens_1'=2,'gx_0'=4,'gx_1'=4,'gy'=4] {'ens_0'}, use_global_device_ids=true, to_apply=%region_1.2 | all-reduce | flops 2 | bytes 16 | tf_op jit(solution)/shard_map/psum | solution.py:39
  363.1 8.9 all-reduce.77
  372.0 8.3 all-reduce.74
  380.3 11.2 %all-reduce.71 = (f32[]{:T(128)}, f32[]{:T(128)}) all-reduce(f32[]{:T(128)} %get-tuple-element.28, f32[]{:T(128)} %get-tuple-element.29), channel_id=1, replica_groups=mesh['ens_0'=2,'ens_1'=2,'gx_0'=4,'gx_1'=4,'gy'=4] {'gx_1'}, use_global_device_ids=true, to_apply=%region_4.5 | all-reduce | flops 2 | bytes 16 | tf_op jit(solution)/shard_map/psum | solution.py:39
  391.5 9.8 all-reduce.68
  404.1 5.4 collective-permute-start.45
  419.2 5.4 collective-permute-start.49
  433.8 6.0 collective-permute-start.53
  448.6 6.7 collective-permute-start.57
  464.1 6.9 collective-permute-start.61
  481.7 6.7 collective-permute-start.65
  499.1 6.7 collective-permute-start.69
  514.6 6.7 collective-permute-start.73
  532.1 6.7 collective-permute-start.77
  555.5 8.4 collective-permute-start.81
  564.0 5.6 multiply_convert_fusion.2
  580.6 7.6 collective-permute-start.85
  588.2 9.6 fusion.1
  601.7 14.7 %all-reduce.79 = (f32[]{:T(128)}, f32[]{:T(128)}) all-reduce(f32[]{:T(128)} %get-tuple-element.9, f32[]{:T(128)} %get-tuple-element.8), channel_id=1, replica_groups=mesh['ens_0'=2,'ens_1'=2,'gx_0'=4,'gx_1'=4,'gy'=4] {'ens_0'}, use_global_device_ids=true, to_apply=%region_17.18 | all-reduce | flops 2 | bytes 16 | tf_op jit(solution)/shard_map/psum | solution.py:39
  616.4 9.8 all-reduce.76
  626.2 8.3 all-reduce.73
  634.6 17.1 %all-reduce.70 = (f32[]{:T(128)}, f32[]{:T(128)}) all-reduce(f32[]{:T(128)} %get-tuple-element.26, f32[]{:T(128)} %get-tuple-element.27), channel_id=1, replica_groups=mesh['ens_0'=2,'ens_1'=2,'gx_0'=4,'gx_1'=4,'gy'=4] {'gx_1'}, use_global_device_ids=true, to_apply=%region_20.21 | all-reduce | flops 2 | bytes 16 | tf_op jit(solution)/shard_map/psum | solution.py:39
  651.7 9.8 all-reduce.67
  668.0 5.4 collective-permute-start.89
  683.1 5.4 collective-permute-start.93
  712.0 5.4 collective-permute-start.101
  726.3 6.2 collective-permute-start.105
  743.2 6.7 collective-permute-start.109
  760.6 6.7 collective-permute-start.113
  776.1 6.8 collective-permute-start.117
  793.7 7.6 collective-permute-start.121
  818.0 8.4 collective-permute-start.125
  826.4 5.5 multiply_convert_fusion.1
  843.0 7.6 collective-permute-start.129
  850.6 9.6 fusion
  864.1 16.1 %all-reduce.78 = (f32[]{:T(128)}, f32[]{:T(128)}) all-reduce(f32[]{:T(128)} %get-tuple-element.11, f32[]{:T(128)} %get-tuple-element.10), channel_id=1, replica_groups=mesh['ens_0'=2,'ens_1'=2,'gx_0'=4,'gx_1'=4,'gy'=4] {'ens_0'}, use_global_device_ids=true, to_apply=%region_33.34 | all-reduce | flops 2 | bytes 16 | tf_op jit(solution)/shard_map/psum | solution.py:39
  880.2 6.2 all-reduce.75
  886.5 8.4 all-reduce.72
  894.9 17.1 %all-reduce.69 = (f32[]{:T(128)}, f32[]{:T(128)}) all-reduce(f32[]{:T(128)} %get-tuple-element.24, f32[]{:T(128)} %get-tuple-element.25), channel_id=1, replica_groups=mesh['ens_0'=2,'ens_1'=2,'gx_0'=4,'gx_1'=4,'gy'=4] {'gx_1'}, use_global_device_ids=true, to_apply=%region_36.37 | all-reduce | flops 2 | bytes 16 | tf_op jit(solution)/shard_map/psum | solution.py:39
  912.0 10.0 all-reduce.66
  927.2 5.7 multiply_convert_fusion
  933.0 6.4 convert_bitcast_fusion
  939.4 9.3 reshape.181
  948.6 5.7 all-to-all-start.1
  955.1 111.1 %all-to-all-done.1 = bf16[64,75,4,128]{3,2,1,0:T(4,128)(2,1)} async-done(((bf16[64,75,4,128]{3,2,1,0:T(4,128)(2,1)}), bf16[64,75,4,128]{3,2,1,0:T(4,128)(2,1)}, u32[]{:S(2)}, u32[]{:S(2)}) %all-to-all-start.1) | async-done | bytes 4915232 | tf_op jit(solution)/shard_map/all_to_all | solution.py:148
  1066.2 7.4 copy.105
  (415 shorter events, 337.4 us)
Async XLA Ops:
  8.5 293.1 %all-to-all-start = ((bf16[1,75,256,128]{3,1,0,2:T(8,128)(2,1)}), bf16[1,75,256,128]{3,1,0,2:T(8,128)(2,1)}, u32[]{:S(2)}, u32[]{:S(2)}) async-start(bf16[1,75,256,128]{3,1,0,2:T(8,128)(2,1)} %copy.72), calls=%async_computation | async-start | bytes 10485760 | tf_op jit(solution)/shard_map/all_to_all | solution.py:107
  21.3 116.4 %collective-permute-start.2 = (bf16[75,1,128]{0,2,1:T(8,128)(2,1)S(1)}, bf16[75,1,128]{0,2,1:T(8,128)(2,1)S(1)}, u32[]{:S(2)}, u32[]{:S(2)}) collective-permute-start(bf16[75,1,128]{0,2,1:T(8,128)(2,1)S(1)} %get-tuple-element.133), channel_id=1, source_target_pairs={{4,0},{8,4},{12,8},{16,12},{20,16},{24,20},{28,24},{32,28},{36,32}... | collective-permute-start | bytes 57608 | tf_op jit(solution)/shard_map/ppermute | solution.py:26
  22.6 115.1 %collective-permute-start.1 = (bf16[75,1,128]{0,2,1:T(8,128)(2,1)S(1)}, bf16[75,1,128]{0,2,1:T(8,128)(2,1)S(1)}, u32[]{:S(2)}, u32[]{:S(2)}) collective-permute-start(bf16[75,1,128]{0,2,1:T(8,128)(2,1)S(1)} %get-tuple-element.132), channel_id=1, source_target_pairs={{0,4},{4,8},{8,12},{12,16},{16,20},{20,24},{24,28},{28,32},{32,36}... | collective-permute-start | bytes 57608 | tf_op jit(solution)/shard_map/ppermute | solution.py:25
  138.0 15.4 %collective-permute-start.6 = (bf16[75,1,128]{0,2,1:T(8,128)(2,1)S(1)}, bf16[75,1,128]{0,2,1:T(8,128)(2,1)S(1)}, u32[]{:S(2)}, u32[]{:S(2)}) collective-permute-start(bf16[75,1,128]{0,2,1:T(8,128)(2,1)S(1)} %get-tuple-element.129), channel_id=1, source_target_pairs={{4,0},{8,4},{12,8},{16,12},{20,16},{24,20},{28,24},{32,28},{36,32}... | collective-permute-start | bytes 57608 | tf_op jit(solution)/shard_map/ppermute | solution.py:26
  153.8 15.4 %collective-permute-start.10 = (bf16[75,1,64]{0,2,1:T(8,128)(2,1)S(1)}, bf16[75,1,64]{0,2,1:T(8,128)(2,1)S(1)}, u32[]{:S(2)}, u32[]{:S(2)}) collective-permute-start(bf16[75,1,64]{0,2,1:T(8,128)(2,1)S(1)} %get-tuple-element.181), channel_id=1, source_target_pairs={{4,0},{8,4},{12,8},{16,12},{20,16},{24,20},{28,24},{32,28},{36,32}... | collective-permute-start | bytes 28808 | tf_op jit(solution)/shard_map/ppermute | solution.py:26
  155.1 14.1 %collective-permute-start.9 = (bf16[75,1,64]{0,2,1:T(8,128)(2,1)S(1)}, bf16[75,1,64]{0,2,1:T(8,128)(2,1)S(1)}, u32[]{:S(2)}, u32[]{:S(2)}) collective-permute-start(bf16[75,1,64]{0,2,1:T(8,128)(2,1)S(1)} %get-tuple-element.180), channel_id=1, source_target_pairs={{0,4},{4,8},{8,12},{12,16},{16,20},{20,24},{24,28},{28,32},{32,36}... | collective-permute-start | bytes 28808 | tf_op jit(solution)/shard_map/ppermute | solution.py:25
  169.3 15.4 %collective-permute-start.14 = (bf16[75,1,64]{0,2,1:T(8,128)(2,1)S(1)}, bf16[75,1,64]{0,2,1:T(8,128)(2,1)S(1)}, u32[]{:S(2)}, u32[]{:S(2)}) collective-permute-start(bf16[75,1,64]{0,2,1:T(8,128)(2,1)S(1)} %get-tuple-element.177), channel_id=1, source_target_pairs={{4,0},{8,4},{12,8},{16,12},{20,16},{24,20},{28,24},{32,28},{36,32}... | collective-permute-start | bytes 28808 | tf_op jit(solution)/shard_map/ppermute | solution.py:26
  170.6 14.1 %collective-permute-start.13 = (bf16[75,1,64]{0,2,1:T(8,128)(2,1)S(1)}, bf16[75,1,64]{0,2,1:T(8,128)(2,1)S(1)}, u32[]{:S(2)}, u32[]{:S(2)}) collective-permute-start(bf16[75,1,64]{0,2,1:T(8,128)(2,1)S(1)} %get-tuple-element.176), channel_id=1, source_target_pairs={{0,4},{4,8},{8,12},{12,16},{16,20},{20,24},{24,28},{28,32},{32,36}... | collective-permute-start | bytes 28808 | tf_op jit(solution)/shard_map/ppermute | solution.py:25
  184.8 17.4 %collective-permute-start.16 = (f32[75,1,32]{0,2,1:T(8,128)S(1)}, f32[75,1,32]{0,2,1:T(8,128)S(1)}, u32[]{:S(2)}, u32[]{:S(2)}) collective-permute-start(f32[75,1,32]{0,2,1:T(8,128)S(1)} %multiply_bitcast_fusion.2), channel_id=1, source_target_pairs={{4,0},{8,4},{12,8},{16,12},{20,16},{24,20},{28,24},{32,28},{36,32}... | collective-permute-start | bytes 28808 | tf_op jit(solution)/shard_map/ppermute | solution.py:26
  186.1 16.1 %collective-permute-start.17 = (f32[75,1,32]{0,2,1:T(8,128)S(1)}, f32[75,1,32]{0,2,1:T(8,128)S(1)}, u32[]{:S(2)}, u32[]{:S(2)}) collective-permute-start(f32[75,1,32]{0,2,1:T(8,128)S(1)} %multiply_bitcast_fusion.2), channel_id=1, source_target_pairs={{0,4},{4,8},{8,12},{12,16},{16,20},{20,24},{24,28},{28,32},{32,36}... | collective-permute-start | bytes 28808 | tf_op jit(solution)/shard_map/ppermute | solution.py:25
  202.2 17.4 %collective-permute-start.20 = (f32[75,1,32]{0,2,1:T(8,128)S(1)}, f32[75,1,32]{0,2,1:T(8,128)S(1)}, u32[]{:S(2)}, u32[]{:S(2)}) collective-permute-start(f32[75,1,32]{0,2,1:T(8,128)S(1)} %fusion.369), channel_id=1, source_target_pairs={{4,0},{8,4},{12,8},{16,12},{20,16},{24,20},{28,24},{32,28},{36,32}... | collective-permute-start | bytes 28808 | tf_op jit(solution)/shard_map/ppermute | solution.py:26
  203.5 16.1 %collective-permute-start.21 = (f32[75,1,32]{0,2,1:T(8,128)S(1)}, f32[75,1,32]{0,2,1:T(8,128)S(1)}, u32[]{:S(2)}, u32[]{:S(2)}) collective-permute-start(f32[75,1,32]{0,2,1:T(8,128)S(1)} %fusion.369), channel_id=1, source_target_pairs={{0,4},{4,8},{8,12},{12,16},{16,20},{20,24},{24,28},{28,32},{32,36}... | collective-permute-start | bytes 28808 | tf_op jit(solution)/shard_map/ppermute | solution.py:25
  219.6 15.4 %collective-permute-start.24 = (f32[75,1,32]{0,2,1:T(8,128)S(1)}, f32[75,1,32]{0,2,1:T(8,128)S(1)}, u32[]{:S(2)}, u32[]{:S(2)}) collective-permute-start(f32[75,1,32]{0,2,1:T(8,128)S(1)} %fusion.360), channel_id=1, source_target_pairs={{4,0},{8,4},{12,8},{16,12},{20,16},{24,20},{28,24},{32,28},{36,32}... | collective-permute-start | bytes 28808 | tf_op jit(solution)/shard_map/ppermute | solution.py:26
  220.9 14.1 %collective-permute-start.25 = (f32[75,1,32]{0,2,1:T(8,128)S(1)}, f32[75,1,32]{0,2,1:T(8,128)S(1)}, u32[]{:S(2)}, u32[]{:S(2)}) collective-permute-start(f32[75,1,32]{0,2,1:T(8,128)S(1)} %fusion.360), channel_id=1, source_target_pairs={{0,4},{4,8},{8,12},{12,16},{16,20},{20,24},{24,28},{28,32},{32,36}... | collective-permute-start | bytes 28808 | tf_op jit(solution)/shard_map/ppermute | solution.py:25
  235.0 17.4 %collective-permute-start.30 = (bf16[75,1,64]{0,2,1:T(8,128)(2,1)S(1)}, bf16[75,1,64]{0,2,1:T(8,128)(2,1)S(1)}, u32[]{:S(2)}, u32[]{:S(2)}) collective-permute-start(bf16[75,1,64]{0,2,1:T(8,128)(2,1)S(1)} %get-tuple-element.173), channel_id=1, source_target_pairs={{4,0},{8,4},{12,8},{16,12},{20,16},{24,20},{28,24},{32,28},{36,32}... | collective-permute-start | bytes 28808 | tf_op jit(solution)/shard_map/ppermute | solution.py:26
  236.3 16.1 %collective-permute-start.29 = (bf16[75,1,64]{0,2,1:T(8,128)(2,1)S(1)}, bf16[75,1,64]{0,2,1:T(8,128)(2,1)S(1)}, u32[]{:S(2)}, u32[]{:S(2)}) collective-permute-start(bf16[75,1,64]{0,2,1:T(8,128)(2,1)S(1)} %get-tuple-element.172), channel_id=1, source_target_pairs={{0,4},{4,8},{8,12},{12,16},{16,20},{20,24},{24,28},{28,32},{32,36}... | collective-permute-start | bytes 28808 | tf_op jit(solution)/shard_map/ppermute | solution.py:25
  252.5 15.4 %collective-permute-start.34 = (bf16[75,1,64]{0,2,1:T(8,128)(2,1)S(1)}, bf16[75,1,64]{0,2,1:T(8,128)(2,1)S(1)}, u32[]{:S(2)}, u32[]{:S(2)}) collective-permute-start(bf16[75,1,64]{0,2,1:T(8,128)(2,1)S(1)} %get-tuple-element.169), channel_id=1, source_target_pairs={{4,0},{8,4},{12,8},{16,12},{20,16},{24,20},{28,24},{32,28},{36,32}... | collective-permute-start | bytes 28808 | tf_op jit(solution)/shard_map/ppermute | solution.py:26
  253.8 14.1 %collective-permute-start.33 = (bf16[75,1,64]{0,2,1:T(8,128)(2,1)S(1)}, bf16[75,1,64]{0,2,1:T(8,128)(2,1)S(1)}, u32[]{:S(2)}, u32[]{:S(2)}) collective-permute-start(bf16[75,1,64]{0,2,1:T(8,128)(2,1)S(1)} %get-tuple-element.168), channel_id=1, source_target_pairs={{0,4},{4,8},{8,12},{12,16},{16,20},{20,24},{24,28},{28,32},{32,36}... | collective-permute-start | bytes 28808 | tf_op jit(solution)/shard_map/ppermute | solution.py:25
  268.1 15.5 %collective-permute-start.38 = (bf16[75,1,128]{0,2,1:T(8,128)(2,1)S(1)}, bf16[75,1,128]{0,2,1:T(8,128)(2,1)S(1)}, u32[]{:S(2)}, u32[]{:S(2)}) collective-permute-start(bf16[75,1,128]{0,2,1:T(8,128)(2,1)S(1)} %get-tuple-element.125), channel_id=1, source_target_pairs={{4,0},{8,4},{12,8},{16,12},{20,16},{24,20},{28,24},{32,28},{36,32}... | collective-permute-start | bytes 57608 | tf_op jit(solution)/shard_map/ppermute | solution.py:26
  269.4 14.2 %collective-permute-start.37 = (bf16[75,1,128]{0,2,1:T(8,128)(2,1)S(1)}, bf16[75,1,128]{0,2,1:T(8,128)(2,1)S(1)}, u32[]{:S(2)}, u32[]{:S(2)}) collective-permute-start(bf16[75,1,128]{0,2,1:T(8,128)(2,1)S(1)} %get-tuple-element.124), channel_id=1, source_target_pairs={{0,4},{4,8},{8,12},{12,16},{16,20},{20,24},{24,28},{28,32},{32,36}... | collective-permute-start | bytes 57608 | tf_op jit(solution)/shard_map/ppermute | solution.py:25
  284.5 15.9 %collective-permute-start.43 = (bf16[75,4,1]{0,2,1:T(2,128)(2,1)S(1)}, bf16[75,4,1]{0,2,1:T(2,128)(2,1)S(1)}, u32[]{:S(2)}, u32[]{:S(2)}) collective-permute-start(bf16[75,4,1]{0,2,1:T(2,128)(2,1)S(1)} %get-tuple-element.123), channel_id=1, source_target_pairs={{1,0},{2,1},{3,2},{5,4},{6,5},{7,6},{9,8},{10,9},{11,10},{13,12},{... | collective-permute-start | bytes 1808 | tf_op jit(solution)/shard_map/ppermute | solution.py:26
  402.8 14.8 %collective-permute-start.46 = (bf16[75,1,128]{0,2,1:T(8,128)(2,1)S(1)}, bf16[75,1,128]{0,2,1:T(8,128)(2,1)S(1)}, u32[]{:S(2)}, u32[]{:S(2)}) collective-permute-start(bf16[75,1,128]{0,2,1:T(8,128)(2,1)S(1)} %get-tuple-element.117), channel_id=1, source_target_pairs={{4,0},{8,4},{12,8},{16,12},{20,16},{24,20},{28,24},{32,28},{36,32}... | collective-permute-start | bytes 57608 | tf_op jit(solution)/shard_map/ppermute | solution.py:26
  417.9 14.2 %collective-permute-start.50 = (bf16[75,1,128]{0,2,1:T(8,128)(2,1)S(1)}, bf16[75,1,128]{0,2,1:T(8,128)(2,1)S(1)}, u32[]{:S(2)}, u32[]{:S(2)}) collective-permute-start(bf16[75,1,128]{0,2,1:T(8,128)(2,1)S(1)} %get-tuple-element.113), channel_id=1, source_target_pairs={{4,0},{8,4},{12,8},{16,12},{20,16},{24,20},{28,24},{32,28},{36,32}... | collective-permute-start | bytes 57608 | tf_op jit(solution)/shard_map/ppermute | solution.py:26
  432.5 14.7 %collective-permute-start.54 = (bf16[75,1,64]{0,2,1:T(8,128)(2,1)S(1)}, bf16[75,1,64]{0,2,1:T(8,128)(2,1)S(1)}, u32[]{:S(2)}, u32[]{:S(2)}) collective-permute-start(bf16[75,1,64]{0,2,1:T(8,128)(2,1)S(1)} %get-tuple-element.165), channel_id=1, source_target_pairs={{4,0},{8,4},{12,8},{16,12},{20,16},{24,20},{28,24},{32,28},{36,32}... | collective-permute-start | bytes 28808 | tf_op jit(solution)/shard_map/ppermute | solution.py:26
  447.3 15.4 %collective-permute-start.58 = (bf16[75,1,64]{0,2,1:T(8,128)(2,1)S(1)}, bf16[75,1,64]{0,2,1:T(8,128)(2,1)S(1)}, u32[]{:S(2)}, u32[]{:S(2)}) collective-permute-start(bf16[75,1,64]{0,2,1:T(8,128)(2,1)S(1)} %get-tuple-element.161), channel_id=1, source_target_pairs={{4,0},{8,4},{12,8},{16,12},{20,16},{24,20},{28,24},{32,28},{36,32}... | collective-permute-start | bytes 28808 | tf_op jit(solution)/shard_map/ppermute | solution.py:26
  448.6 14.1 %collective-permute-start.57 = (bf16[75,1,64]{0,2,1:T(8,128)(2,1)S(1)}, bf16[75,1,64]{0,2,1:T(8,128)(2,1)S(1)}, u32[]{:S(2)}, u32[]{:S(2)}) collective-permute-start(bf16[75,1,64]{0,2,1:T(8,128)(2,1)S(1)} %get-tuple-element.160), channel_id=1, source_target_pairs={{0,4},{4,8},{8,12},{12,16},{16,20},{20,24},{24,28},{28,32},{32,36}... | collective-permute-start | bytes 28808 | tf_op jit(solution)/shard_map/ppermute | solution.py:25
  462.8 17.6 %collective-permute-start.60 = (f32[75,1,32]{0,2,1:T(8,128)S(1)}, f32[75,1,32]{0,2,1:T(8,128)S(1)}, u32[]{:S(2)}, u32[]{:S(2)}) collective-permute-start(f32[75,1,32]{0,2,1:T(8,128)S(1)} %multiply_bitcast_fusion.1), channel_id=1, source_target_pairs={{4,0},{8,4},{12,8},{16,12},{20,16},{24,20},{28,24},{32,28},{36,32}... | collective-permute-start | bytes 28808 | tf_op jit(solution)/shard_map/ppermute | solution.py:26
  464.1 16.3 %collective-permute-start.61 = (f32[75,1,32]{0,2,1:T(8,128)S(1)}, f32[75,1,32]{0,2,1:T(8,128)S(1)}, u32[]{:S(2)}, u32[]{:S(2)}) collective-permute-start(f32[75,1,32]{0,2,1:T(8,128)S(1)} %multiply_bitcast_fusion.1), channel_id=1, source_target_pairs={{0,4},{4,8},{8,12},{12,16},{16,20},{20,24},{24,28},{28,32},{32,36}... | collective-permute-start | bytes 28808 | tf_op jit(solution)/shard_map/ppermute | solution.py:25
  480.4 17.4 %collective-permute-start.64 = (f32[75,1,32]{0,2,1:T(8,128)S(1)}, f32[75,1,32]{0,2,1:T(8,128)S(1)}, u32[]{:S(2)}, u32[]{:S(2)}) collective-permute-start(f32[75,1,32]{0,2,1:T(8,128)S(1)} %fusion.341), channel_id=1, source_target_pairs={{4,0},{8,4},{12,8},{16,12},{20,16},{24,20},{28,24},{32,28},{36,32}... | collective-permute-start | bytes 28808 | tf_op jit(solution)/shard_map/ppermute | solution.py:26
  481.7 16.1 %collective-permute-start.65 = (f32[75,1,32]{0,2,1:T(8,128)S(1)}, f32[75,1,32]{0,2,1:T(8,128)S(1)}, u32[]{:S(2)}, u32[]{:S(2)}) collective-permute-start(f32[75,1,32]{0,2,1:T(8,128)S(1)} %fusion.341), channel_id=1, source_target_pairs={{0,4},{4,8},{8,12},{12,16},{16,20},{20,24},{24,28},{28,32},{32,36}... | collective-permute-start | bytes 28808 | tf_op jit(solution)/shard_map/ppermute | solution.py:25
  497.8 15.4 %collective-permute-start.68 = (f32[75,1,32]{0,2,1:T(8,128)S(1)}, f32[75,1,32]{0,2,1:T(8,128)S(1)}, u32[]{:S(2)}, u32[]{:S(2)}) collective-permute-start(f32[75,1,32]{0,2,1:T(8,128)S(1)} %fusion.332), channel_id=1, source_target_pairs={{4,0},{8,4},{12,8},{16,12},{20,16},{24,20},{28,24},{32,28},{36,32}... | collective-permute-start | bytes 28808 | tf_op jit(solution)/shard_map/ppermute | solution.py:26
  499.1 14.1 %collective-permute-start.69 = (f32[75,1,32]{0,2,1:T(8,128)S(1)}, f32[75,1,32]{0,2,1:T(8,128)S(1)}, u32[]{:S(2)}, u32[]{:S(2)}) collective-permute-start(f32[75,1,32]{0,2,1:T(8,128)S(1)} %fusion.332), channel_id=1, source_target_pairs={{0,4},{4,8},{8,12},{12,16},{16,20},{20,24},{24,28},{28,32},{32,36}... | collective-permute-start | bytes 28808 | tf_op jit(solution)/shard_map/ppermute | solution.py:25
  513.3 17.4 %collective-permute-start.74 = (bf16[75,1,64]{0,2,1:T(8,128)(2,1)S(1)}, bf16[75,1,64]{0,2,1:T(8,128)(2,1)S(1)}, u32[]{:S(2)}, u32[]{:S(2)}) collective-permute-start(bf16[75,1,64]{0,2,1:T(8,128)(2,1)S(1)} %get-tuple-element.157), channel_id=1, source_target_pairs={{4,0},{8,4},{12,8},{16,12},{20,16},{24,20},{28,24},{32,28},{36,32}... | collective-permute-start | bytes 28808 | tf_op jit(solution)/shard_map/ppermute | solution.py:26
  514.6 16.1 %collective-permute-start.73 = (bf16[75,1,64]{0,2,1:T(8,128)(2,1)S(1)}, bf16[75,1,64]{0,2,1:T(8,128)(2,1)S(1)}, u32[]{:S(2)}, u32[]{:S(2)}) collective-permute-start(bf16[75,1,64]{0,2,1:T(8,128)(2,1)S(1)} %get-tuple-element.156), channel_id=1, source_target_pairs={{0,4},{4,8},{8,12},{12,16},{16,20},{20,24},{24,28},{28,32},{32,36}... | collective-permute-start | bytes 28808 | tf_op jit(solution)/shard_map/ppermute | solution.py:25
  530.8 15.4 %collective-permute-start.78 = (bf16[75,1,64]{0,2,1:T(8,128)(2,1)S(1)}, bf16[75,1,64]{0,2,1:T(8,128)(2,1)S(1)}, u32[]{:S(2)}, u32[]{:S(2)}) collective-permute-start(bf16[75,1,64]{0,2,1:T(8,128)(2,1)S(1)} %get-tuple-element.153), channel_id=1, source_target_pairs={{4,0},{8,4},{12,8},{16,12},{20,16},{24,20},{28,24},{32,28},{36,32}... | collective-permute-start | bytes 28808 | tf_op jit(solution)/shard_map/ppermute | solution.py:26
  532.1 14.1 %collective-permute-start.77 = (bf16[75,1,64]{0,2,1:T(8,128)(2,1)S(1)}, bf16[75,1,64]{0,2,1:T(8,128)(2,1)S(1)}, u32[]{:S(2)}, u32[]{:S(2)}) collective-permute-start(bf16[75,1,64]{0,2,1:T(8,128)(2,1)S(1)} %get-tuple-element.152), channel_id=1, source_target_pairs={{0,4},{4,8},{8,12},{12,16},{16,20},{20,24},{24,28},{28,32},{32,36}... | collective-permute-start | bytes 28808 | tf_op jit(solution)/shard_map/ppermute | solution.py:25
  548.4 21.2 %collective-permute-start.83 = (bf16[75,4,1]{0,2,1:T(2,128)(2,1)}, bf16[75,4,1]{0,2,1:T(2,128)(2,1)S(1)}, u32[]{:S(2)}, u32[]{:S(2)}) collective-permute-start(bf16[75,4,1]{0,2,1:T(2,128)(2,1)} %get-tuple-element.111), channel_id=1, source_target_pairs={{1,0},{2,1},{3,2},{5,4},{6,5},{7,6},{9,8},{10,9},{11,10},{13,12},{... | collective-permute-start | bytes 1808 | tf_op jit(solution)/shard_map/ppermute | solution.py:26
  550.3 19.3 %collective-permute-start.80 = (bf16[75,4,1]{0,2,1:T(2,128)(2,1)}, bf16[75,4,1]{0,2,1:T(2,128)(2,1)}, u32[]{:S(2)}, u32[]{:S(2)}) collective-permute-start(bf16[75,4,1]{0,2,1:T(2,128)(2,1)} %get-tuple-element.110), channel_id=1, source_target_pairs={{0,1},{1,2},{2,3},{4,5},{5,6},{6,7},{8,9},{9,10},{10,11},{12,13},{... | collective-permute-start | bytes 1808 | tf_op jit(solution)/shard_map/ppermute | solution.py:25
  554.2 15.4 %collective-permute-start.82 = (bf16[75,1,128]{0,2,1:T(8,128)(2,1)}, bf16[75,1,128]{0,2,1:T(8,128)(2,1)S(1)}, u32[]{:S(2)}, u32[]{:S(2)}) collective-permute-start(bf16[75,1,128]{0,2,1:T(8,128)(2,1)} %get-tuple-element.109), channel_id=1, source_target_pairs={{4,0},{8,4},{12,8},{16,12},{20,16},{24,20},{28,24},{32,28},{36,32}... | collective-permute-start | bytes 57608 | tf_op jit(solution)/shard_map/ppermute | solution.py:26
  573.5 25.4 %collective-permute-start.87 = (bf16[75,4,1]{0,2,1:T(2,128)(2,1)}, bf16[75,4,1]{0,2,1:T(2,128)(2,1)S(1)}, u32[]{:S(2)}, u32[]{:S(2)}) collective-permute-start(bf16[75,4,1]{0,2,1:T(2,128)(2,1)} %get-tuple-element.107), channel_id=1, source_target_pairs={{1,0},{2,1},{3,2},{5,4},{6,5},{7,6},{9,8},{10,9},{11,10},{13,12},{... | collective-permute-start | bytes 1808 | tf_op jit(solution)/shard_map/ppermute | solution.py:26
  575.9 23.0 %collective-permute-start.84 = (bf16[75,4,1]{0,2,1:T(2,128)(2,1)}, bf16[75,4,1]{0,2,1:T(2,128)(2,1)}, u32[]{:S(2)}, u32[]{:S(2)}) collective-permute-start(bf16[75,4,1]{0,2,1:T(2,128)(2,1)} %get-tuple-element.106), channel_id=1, source_target_pairs={{0,1},{1,2},{2,3},{4,5},{5,6},{6,7},{8,9},{9,10},{10,11},{12,13},{... | collective-permute-start | bytes 1808 | tf_op jit(solution)/shard_map/ppermute | solution.py:25
  579.3 19.6 %collective-permute-start.86 = (bf16[75,1,128]{0,2,1:T(8,128)(2,1)}, bf16[75,1,128]{0,2,1:T(8,128)(2,1)S(1)}, u32[]{:S(2)}, u32[]{:S(2)}) collective-permute-start(bf16[75,1,128]{0,2,1:T(8,128)(2,1)} %get-tuple-element.105), channel_id=1, source_target_pairs={{4,0},{8,4},{12,8},{16,12},{20,16},{24,20},{28,24},{32,28},{36,32}... | collective-permute-start | bytes 57608 | tf_op jit(solution)/shard_map/ppermute | solution.py:26
  580.6 18.3 %collective-permute-start.85 = (bf16[75,1,128]{0,2,1:T(8,128)(2,1)}, bf16[75,1,128]{0,2,1:T(8,128)(2,1)}, u32[]{:S(2)}, u32[]{:S(2)}) collective-permute-start(bf16[75,1,128]{0,2,1:T(8,128)(2,1)} %get-tuple-element.104), channel_id=1, source_target_pairs={{0,4},{4,8},{8,12},{12,16},{16,20},{20,24},{24,28},{28,32},{32,36}... | collective-permute-start | bytes 57608 | tf_op jit(solution)/shard_map/ppermute | solution.py:25
  666.7 14.8 %collective-permute-start.90 = (bf16[75,1,128]{0,2,1:T(8,128)(2,1)S(1)}, bf16[75,1,128]{0,2,1:T(8,128)(2,1)S(1)}, u32[]{:S(2)}, u32[]{:S(2)}) collective-permute-start(bf16[75,1,128]{0,2,1:T(8,128)(2,1)S(1)} %get-tuple-element.101), channel_id=1, source_target_pairs={{4,0},{8,4},{12,8},{16,12},{20,16},{24,20},{28,24},{32,28},{36,32}... | collective-permute-start | bytes 57608 | tf_op jit(solution)/shard_map/ppermute | solution.py:26
  681.8 14.2 %collective-permute-start.94 = (bf16[75,1,128]{0,2,1:T(8,128)(2,1)S(1)}, bf16[75,1,128]{0,2,1:T(8,128)(2,1)S(1)}, u32[]{:S(2)}, u32[]{:S(2)}) collective-permute-start(bf16[75,1,128]{0,2,1:T(8,128)(2,1)S(1)} %get-tuple-element.97), channel_id=1, source_target_pairs={{4,0},{8,4},{12,8},{16,12},{20,16},{24,20},{28,24},{32,28},{36,32}... | collective-permute-start | bytes 57608 | tf_op jit(solution)/shard_map/ppermute | solution.py:26
  696.4 14.2 %collective-permute-start.98 = (bf16[75,1,64]{0,2,1:T(8,128)(2,1)S(1)}, bf16[75,1,64]{0,2,1:T(8,128)(2,1)S(1)}, u32[]{:S(2)}, u32[]{:S(2)}) collective-permute-start(bf16[75,1,64]{0,2,1:T(8,128)(2,1)S(1)} %get-tuple-element.149), channel_id=1, source_target_pairs={{4,0},{8,4},{12,8},{16,12},{20,16},{24,20},{28,24},{32,28},{36,32}... | collective-permute-start | bytes 28808 | tf_op jit(solution)/shard_map/ppermute | solution.py:26
  710.7 14.2 %collective-permute-start.102 = (bf16[75,1,64]{0,2,1:T(8,128)(2,1)S(1)}, bf16[75,1,64]{0,2,1:T(8,128)(2,1)S(1)}, u32[]{:S(2)}, u32[]{:S(2)}) collective-permute-start(bf16[75,1,64]{0,2,1:T(8,128)(2,1)S(1)} %get-tuple-element.145), channel_id=1, source_target_pairs={{4,0},{8,4},{12,8},{16,12},{20,16},{24,20},{28,24},{32,28},{36,32}... | collective-permute-start | bytes 28808 | tf_op jit(solution)/shard_map/ppermute | solution.py:26
  725.0 16.9 %collective-permute-start.104 = (f32[75,1,32]{0,2,1:T(8,128)S(1)}, f32[75,1,32]{0,2,1:T(8,128)S(1)}, u32[]{:S(2)}, u32[]{:S(2)}) collective-permute-start(f32[75,1,32]{0,2,1:T(8,128)S(1)} %multiply_bitcast_fusion), channel_id=1, source_target_pairs={{4,0},{8,4},{12,8},{16,12},{20,16},{24,20},{28,24},{32,28},{36,32}... | collective-permute-start | bytes 28808 | tf_op jit(solution)/shard_map/ppermute | solution.py:26
  726.3 15.6 %collective-permute-start.105 = (f32[75,1,32]{0,2,1:T(8,128)S(1)}, f32[75,1,32]{0,2,1:T(8,128)S(1)}, u32[]{:S(2)}, u32[]{:S(2)}) collective-permute-start(f32[75,1,32]{0,2,1:T(8,128)S(1)} %multiply_bitcast_fusion), channel_id=1, source_target_pairs={{0,4},{4,8},{8,12},{12,16},{16,20},{20,24},{24,28},{28,32},{32,36}... | collective-permute-start | bytes 28808 | tf_op jit(solution)/shard_map/ppermute | solution.py:25
  741.9 17.4 %collective-permute-start.108 = (f32[75,1,32]{0,2,1:T(8,128)S(1)}, f32[75,1,32]{0,2,1:T(8,128)S(1)}, u32[]{:S(2)}, u32[]{:S(2)}) collective-permute-start(f32[75,1,32]{0,2,1:T(8,128)S(1)} %fusion.313), channel_id=1, source_target_pairs={{4,0},{8,4},{12,8},{16,12},{20,16},{24,20},{28,24},{32,28},{36,32}... | collective-permute-start | bytes 28808 | tf_op jit(solution)/shard_map/ppermute | solution.py:26
  743.2 16.1 %collective-permute-start.109 = (f32[75,1,32]{0,2,1:T(8,128)S(1)}, f32[75,1,32]{0,2,1:T(8,128)S(1)}, u32[]{:S(2)}, u32[]{:S(2)}) collective-permute-start(f32[75,1,32]{0,2,1:T(8,128)S(1)} %fusion.313), channel_id=1, source_target_pairs={{0,4},{4,8},{8,12},{12,16},{16,20},{20,24},{24,28},{28,32},{32,36}... | collective-permute-start | bytes 28808 | tf_op jit(solution)/shard_map/ppermute | solution.py:25
  759.3 15.4 %collective-permute-start.112 = (f32[75,1,32]{0,2,1:T(8,128)S(1)}, f32[75,1,32]{0,2,1:T(8,128)S(1)}, u32[]{:S(2)}, u32[]{:S(2)}) collective-permute-start(f32[75,1,32]{0,2,1:T(8,128)S(1)} %fusion.304), channel_id=1, source_target_pairs={{4,0},{8,4},{12,8},{16,12},{20,16},{24,20},{28,24},{32,28},{36,32}... | collective-permute-start | bytes 28808 | tf_op jit(solution)/shard_map/ppermute | solution.py:26
  774.8 17.5 %collective-permute-start.118 = (bf16[75,1,64]{0,2,1:T(8,128)(2,1)S(1)}, bf16[75,1,64]{0,2,1:T(8,128)(2,1)S(1)}, u32[]{:S(2)}, u32[]{:S(2)}) collective-permute-start(bf16[75,1,64]{0,2,1:T(8,128)(2,1)S(1)} %get-tuple-element.141), channel_id=1, source_target_pairs={{4,0},{8,4},{12,8},{16,12},{20,16},{24,20},{28,24},{32,28},{36,32}... | collective-permute-start | bytes 28808 | tf_op jit(solution)/shard_map/ppermute | solution.py:26
  776.1 16.2 %collective-permute-start.117 = (bf16[75,1,64]{0,2,1:T(8,128)(2,1)S(1)}, bf16[75,1,64]{0,2,1:T(8,128)(2,1)S(1)}, u32[]{:S(2)}, u32[]{:S(2)}) collective-permute-start(bf16[75,1,64]{0,2,1:T(8,128)(2,1)S(1)} %get-tuple-element.140), channel_id=1, source_target_pairs={{0,4},{4,8},{8,12},{12,16},{16,20},{20,24},{24,28},{28,32},{32,36}... | collective-permute-start | bytes 28808 | tf_op jit(solution)/shard_map/ppermute | solution.py:25
  792.4 16.3 %collective-permute-start.122 = (bf16[75,1,64]{0,2,1:T(8,128)(2,1)S(1)}, bf16[75,1,64]{0,2,1:T(8,128)(2,1)S(1)}, u32[]{:S(2)}, u32[]{:S(2)}) collective-permute-start(bf16[75,1,64]{0,2,1:T(8,128)(2,1)S(1)} %get-tuple-element.137), channel_id=1, source_target_pairs={{4,0},{8,4},{12,8},{16,12},{20,16},{24,20},{28,24},{32,28},{36,32}... | collective-permute-start | bytes 28808 | tf_op jit(solution)/shard_map/ppermute | solution.py:26
  793.7 15.0 %collective-permute-start.121 = (bf16[75,1,64]{0,2,1:T(8,128)(2,1)S(1)}, bf16[75,1,64]{0,2,1:T(8,128)(2,1)S(1)}, u32[]{:S(2)}, u32[]{:S(2)}) collective-permute-start(bf16[75,1,64]{0,2,1:T(8,128)(2,1)S(1)} %get-tuple-element.136), channel_id=1, source_target_pairs={{0,4},{4,8},{8,12},{12,16},{16,20},{20,24},{24,28},{28,32},{32,36}... | collective-permute-start | bytes 28808 | tf_op jit(solution)/shard_map/ppermute | solution.py:25
  810.8 21.1 %collective-permute-start.127 = (bf16[75,4,1]{0,2,1:T(2,128)(2,1)}, bf16[75,4,1]{0,2,1:T(2,128)(2,1)S(1)}, u32[]{:S(2)}, u32[]{:S(2)}) collective-permute-start(bf16[75,4,1]{0,2,1:T(2,128)(2,1)} %get-tuple-element.95), channel_id=1, source_target_pairs={{1,0},{2,1},{3,2},{5,4},{6,5},{7,6},{9,8},{10,9},{11,10},{13,12},{... | collective-permute-start | bytes 1808 | tf_op jit(solution)/shard_map/ppermute | solution.py:26
  812.7 19.2 %collective-permute-start.124 = (bf16[75,4,1]{0,2,1:T(2,128)(2,1)}, bf16[75,4,1]{0,2,1:T(2,128)(2,1)}, u32[]{:S(2)}, u32[]{:S(2)}) collective-permute-start(bf16[75,4,1]{0,2,1:T(2,128)(2,1)} %get-tuple-element.94), channel_id=1, source_target_pairs={{0,1},{1,2},{2,3},{4,5},{5,6},{6,7},{8,9},{9,10},{10,11},{12,13},{... | collective-permute-start | bytes 1808 | tf_op jit(solution)/shard_map/ppermute | solution.py:25
  816.7 15.3 %collective-permute-start.126 = (bf16[75,1,128]{0,2,1:T(8,128)(2,1)}, bf16[75,1,128]{0,2,1:T(8,128)(2,1)S(1)}, u32[]{:S(2)}, u32[]{:S(2)}) collective-permute-start(bf16[75,1,128]{0,2,1:T(8,128)(2,1)} %get-tuple-element.93), channel_id=1, source_target_pairs={{4,0},{8,4},{12,8},{16,12},{20,16},{24,20},{28,24},{32,28},{36,32}... | collective-permute-start | bytes 57608 | tf_op jit(solution)/shard_map/ppermute | solution.py:26
  835.9 25.4 %collective-permute-start.131 = (bf16[75,4,1]{0,2,1:T(2,128)(2,1)}, bf16[75,4,1]{0,2,1:T(2,128)(2,1)S(1)}, u32[]{:S(2)}, u32[]{:S(2)}) collective-permute-start(bf16[75,4,1]{0,2,1:T(2,128)(2,1)} %get-tuple-element.91), channel_id=1, source_target_pairs={{1,0},{2,1},{3,2},{5,4},{6,5},{7,6},{9,8},{10,9},{11,10},{13,12},{... | collective-permute-start | bytes 1808 | tf_op jit(solution)/shard_map/ppermute | solution.py:26
  838.3 23.0 %collective-permute-start.128 = (bf16[75,4,1]{0,2,1:T(2,128)(2,1)}, bf16[75,4,1]{0,2,1:T(2,128)(2,1)}, u32[]{:S(2)}, u32[]{:S(2)}) collective-permute-start(bf16[75,4,1]{0,2,1:T(2,128)(2,1)} %get-tuple-element.90), channel_id=1, source_target_pairs={{0,1},{1,2},{2,3},{4,5},{5,6},{6,7},{8,9},{9,10},{10,11},{12,13},{... | collective-permute-start | bytes 1808 | tf_op jit(solution)/shard_map/ppermute | solution.py:25
  841.7 19.6 %collective-permute-start.130 = (bf16[75,1,128]{0,2,1:T(8,128)(2,1)}, bf16[75,1,128]{0,2,1:T(8,128)(2,1)S(1)}, u32[]{:S(2)}, u32[]{:S(2)}) collective-permute-start(bf16[75,1,128]{0,2,1:T(8,128)(2,1)} %get-tuple-element.89), channel_id=1, source_target_pairs={{4,0},{8,4},{12,8},{16,12},{20,16},{24,20},{28,24},{32,28},{36,32}... | collective-permute-start | bytes 57608 | tf_op jit(solution)/shard_map/ppermute | solution.py:26
  843.0 18.3 %collective-permute-start.129 = (bf16[75,1,128]{0,2,1:T(8,128)(2,1)}, bf16[75,1,128]{0,2,1:T(8,128)(2,1)}, u32[]{:S(2)}, u32[]{:S(2)}) collective-permute-start(bf16[75,1,128]{0,2,1:T(8,128)(2,1)} %get-tuple-element.88), channel_id=1, source_target_pairs={{0,4},{4,8},{8,12},{12,16},{16,20},{20,24},{24,28},{28,32},{32,36}... | collective-permute-start | bytes 57608 | tf_op jit(solution)/shard_map/ppermute | solution.py:25
  948.6 117.5 %all-to-all-start.1 = ((bf16[64,75,4,128]{3,2,1,0:T(4,128)(2,1)}), bf16[64,75,4,128]{3,2,1,0:T(4,128)(2,1)}, u32[]{:S(2)}, u32[]{:S(2)}) async-start(bf16[64,75,4,128]{3,2,1,0:T(4,128)(2,1)} %reshape.181), calls=%async_computation.1 | async-start | bytes 9830400 | tf_op jit(solution)/shard_map/all_to_all | solution.py:148
  (83 other events, 1319.2 us)
where the time goes:
time: 1090 us; the launch traced here: 1070 us
  starting transfers between devices  471 us (43%)
  waiting for transfers between devices  274 us (25%)
  blocking collectives  178 us (16%)
  local copies, waits for them, and re-layouts  57.6 us (5%)
  other arithmetic  45 us (4%)
  matrix products  34.7 us (3%)
  between operations  12.9 us (1%)
    ppermute x66, starting transfers between devices, padded_2(): lax.ppermute(last, axis, up)  332 us
    psum x15, blocking collectives, by_axis(): x = lax.psum(x, axis)  178 us
    ppermute x66, waiting for transfers between devices, padded_2(): lax.ppermute(leading, axis, [(b, a) for a, b in up])  127 us
    ppermute x66, starting transfers between devices, padded_2(): lax.ppermute(leading, axis, [(b, a) for a, b in up])  122 us
    all_to_all x1, waiting for transfers between devices, local(): lax.all_to_all(final, ENS_GX, split_axis=0, concat_axis=2, tiled=True)  111 us
    ppermute x66, waiting for transfers between devices, padded_2(): lax.ppermute(last, axis, up)  36.1 us
    dot_general x4, matrix products, member_products(): jnp.einsum('ij,kjc->kic', spread, flat, preferred_element_type=jnp.float32)  34.7 us
    convert_element_type x4, other arithmetic, member_products(): product = (tiles * masked).astype(jnp.bfloat16)  22.4 us
  transfers between devices with their start and end apart: 134, of which 31 were waited for; matrix products, arithmetic and copies ran while one was open for 4% of the time, Pallas kernels for 0%

commit v1 on v0

--- a/solution.py
+++ b/solution.py
@@ -36,7 +36,7 @@
 
 def by_axis(x, axes):
     for axis in axes:
-        x = lax.psum(x, axis)
+        x = jnp.sum(lax.all_gather(x, axis), axis=0)
     return x
 
 

time: 1090 us -> 1140 us (1.046)
  local copies, waits for them, and re-layouts: 57.6 us -> 103 us
  other arithmetic: 45 us -> 63.2 us
  blocking collectives: 178 us -> 166 us
    psum x15 -> x0, blocking collectives: 178 us -> none  [by_axis(): x = lax.psum(x, axis)]
    unnamed x0 -> x15, blocking collectives: none -> 166 us
    unnamed x31 -> x106, local copies, waits for them, and re-layouts: 10.1 us -> 55.3 us
    reduce_sum x0 -> x30, other arithmetic: none -> 18.2 us  [by_axis(): x = jnp.sum(lax.all_gather(x, axis), axis=0)]
  transfers between devices with their start and end apart: 134 -> 134, of which waited for: 31 -> 30; matrix products, arithmetic and copies ran while one was open for 4% -> 4% of each run, Pallas kernels for 0% -> 0%
where the time goes in v1:
time: 1140 us; the launch traced here: 1120 us
  starting transfers between devices  470 us (41%)
  waiting for transfers between devices  275 us (24%)
  blocking collectives  166 us (15%)
  local copies, waits for them, and re-layouts  103 us (9%)
  other arithmetic  63.2 us (6%)
  matrix products  34.7 us (3%)
  between operations  13.3 us (1%)
    ppermute x66, starting transfers between devices, padded_2(): lax.ppermute(last, axis, up)  329 us
    unnamed x15, blocking collectives  166 us
    ppermute x66, waiting for transfers between devices, padded_2(): lax.ppermute(leading, axis, [(b, a) for a, b in up])  127 us
    ppermute x66, starting transfers between devices, padded_2(): lax.ppermute(leading, axis, [(b, a) for a, b in up])  123 us
    all_to_all x1, waiting for transfers between devices, local(): lax.all_to_all(final, ENS_GX, split_axis=0, concat_axis=2, tiled=True)  111 us
    unnamed x106, local copies, waits for them, and re-layouts  55.3 us
    ppermute x66, waiting for transfers between devices, padded_2(): lax.ppermute(last, axis, up)  36 us
    dot_general x4, matrix products, member_products(): jnp.einsum('ij,kjc->kic', spread, flat, preferred_element_type=jnp.float32)  34.7 us
  transfers between devices with their start and end apart: 134, of which 30 were waited for; matrix products, arithmetic and copies ran while one was open for 4% of the time, Pallas kernels for 0%

profile of v1, /device:TPU:8, one launch (start us, length us, event | category | flops | bytes accessed | tf_op | source)
XLA Modules:
  0.0 1124.3 jit_solution(243036867034139875)
XLA Ops:
  0.6 8.0 copy.72
  8.7 12.3 %all-to-all-start = ((bf16[1,75,256,128]{3,1,0,2:T(8,128)(2,1)}), bf16[1,75,256,128]{3,1,0,2:T(8,128)(2,1)}, u32[]{:S(2)}, u32[]{:S(2)}) async-start(bf16[1,75,256,128]{3,1,0,2:T(8,128)(2,1)} %copy.72), calls=%async_computation | async-start | bytes 10485760 | tf_op jit(solution)/shard_map/all_to_all | solution.py:107
  22.9 5.4 collective-permute-start.1
  36.2 101.6 %collective-permute-done.2 = bf16[75,1,128]{0,2,1:T(8,128)(2,1)S(1)} collective-permute-done((bf16[75,1,128]{0,2,1:T(8,128)(2,1)S(1)}, bf16[75,1,128]{0,2,1:T(8,128)(2,1)S(1)}, u32[]{:S(2)}, u32[]{:S(2)}) %collective-permute-start.2) | collective-permute-done | bytes 19232 | tf_op jit(solution)/shard_map/ppermute | solution.py:26
  139.4 6.0 collective-permute-start.5
  155.1 6.7 collective-permute-start.9
  170.5 6.7 collective-permute-start.13
  186.1 6.7 collective-permute-start.17
  203.5 6.7 collective-permute-start.21
  220.9 6.7 collective-permute-start.25
  236.3 6.7 collective-permute-start.29
  259.7 6.7 collective-permute-start.33
  269.3 6.7 collective-permute-start.37
  285.7 7.6 collective-permute-start.41
  302.2 8.8 copy.131
  311.0 12.5 %reshape.178 = f32[64,75,512]{2,0,1:T(8,128)} reshape(f32[64,1,75,4,128]{4,3,0,2,1:T(4,128)} %bitcast.122) | data formatting | bytes 19660800 | tf_op jit(solution)/shard_map/convert_element_type | solution.py:113
  323.5 5.6 multiply_convert_fusion.3
  330.1 9.0 fusion.2
  343.6 16.1 %all-reduce.110 = (f32[2]{0:T(128)S(1)}, f32[2]{0:T(128)S(1)}) all-reduce(f32[2]{0:T(128)S(1)} %dynamic-update-slice, f32[2]{0:T(128)S(1)} %dynamic-update-slice.5), channel_id=1, replica_groups=mesh['ens_0'=2,'ens_1'=2,'gx_0'=4,'gx_1'=4,'gy'=4] {'ens_0'}, use_global_device_ids=true, to_apply=%add.66 | all-reduce | flops 4 | bytes 32
  364.3 7.3 all-reduce.107
  376.4 7.7 all-reduce.104
  388.7 16.8 %all-reduce.101 = (f32[4]{0:T(128)S(1)}, f32[4]{0:T(128)S(1)}) all-reduce(f32[4]{0:T(128)S(1)} %dynamic-update-slice.3, f32[4]{0:T(128)S(1)} %dynamic-update-slice.8), channel_id=1, replica_groups=mesh['ens_0'=2,'ens_1'=2,'gx_0'=4,'gx_1'=4,'gy'=4] {'gx_1'}, use_global_device_ids=true, to_apply=%add.69 | all-reduce | flops 8 | bytes 64
  409.4 9.1 all-reduce.98
  422.5 5.4 collective-permute-start.45
  439.4 5.4 collective-permute-start.49
  454.1 5.4 collective-permute-start.53
  468.3 5.4 collective-permute-start.57
  482.6 6.2 collective-permute-start.61
  499.6 6.7 collective-permute-start.65
  517.0 6.7 collective-permute-start.69
  532.4 6.8 collective-permute-start.73
  550.0 7.6 collective-permute-start.77
  574.3 8.4 collective-permute-start.81
  582.8 5.6 multiply_convert_fusion.2
  599.4 7.6 collective-permute-start.85
  607.0 9.6 fusion.1
  623.0 15.4 %all-reduce.109 = (f32[2]{0:T(128)S(1)}, f32[2]{0:T(128)S(1)}) all-reduce(f32[2]{0:T(128)S(1)} %dynamic-update-slice.10, f32[2]{0:T(128)S(1)} %dynamic-update-slice.15), channel_id=1, replica_groups=mesh['ens_0'=2,'ens_1'=2,'gx_0'=4,'gx_1'=4,'gy'=4] {'ens_0'}, use_global_device_ids=true, to_apply=%add.76 | all-reduce | flops 4 | bytes 32
  642.3 5.6 all-reduce.106
  652.4 7.7 all-reduce.103
  664.1 16.5 %all-reduce.100 = (f32[4]{0:T(128)S(1)}, f32[4]{0:T(128)S(1)}) all-reduce(f32[4]{0:T(128)S(1)} %dynamic-update-slice.13, f32[4]{0:T(128)S(1)} %dynamic-update-slice.18), channel_id=1, replica_groups=mesh['ens_0'=2,'ens_1'=2,'gx_0'=4,'gx_1'=4,'gy'=4] {'gx_1'}, use_global_device_ids=true, to_apply=%add.79 | all-reduce | flops 8 | bytes 64
  684.5 9.1 all-reduce.97
  701.7 5.4 collective-permute-start.89
  716.7 5.4 collective-permute-start.93
  745.6 5.4 collective-permute-start.101
  760.0 6.2 collective-permute-start.105
  776.9 6.7 collective-permute-start.109
  794.3 6.7 collective-permute-start.113
  809.8 6.8 collective-permute-start.117
  827.4 7.6 collective-permute-start.121
  851.6 8.4 collective-permute-start.125
  860.1 5.6 multiply_convert_fusion.1
  876.7 7.7 collective-permute-start.129
  884.4 9.6 fusion
  900.6 15.4 %all-reduce.108 = (f32[2]{0:T(128)S(1)}, f32[2]{0:T(128)S(1)}) all-reduce(f32[2]{0:T(128)S(1)} %dynamic-update-slice.20, f32[2]{0:T(128)S(1)} %dynamic-update-slice.25), channel_id=1, replica_groups=mesh['ens_0'=2,'ens_1'=2,'gx_0'=4,'gx_1'=4,'gy'=4] {'ens_0'}, use_global_device_ids=true, to_apply=%add.86 | all-reduce | flops 4 | bytes 32
  920.0 5.6 all-reduce.105
  929.7 7.7 all-reduce.102
  941.4 16.5 %all-reduce.99 = (f32[4]{0:T(128)S(1)}, f32[4]{0:T(128)S(1)}) all-reduce(f32[4]{0:T(128)S(1)} %dynamic-update-slice.23, f32[4]{0:T(128)S(1)} %dynamic-update-slice.28), channel_id=1, replica_groups=mesh['ens_0'=2,'ens_1'=2,'gx_0'=4,'gx_1'=4,'gy'=4] {'gx_1'}, use_global_device_ids=true, to_apply=%add.89 | all-reduce | flops 8 | bytes 64
  961.8 9.3 all-reduce.96
  977.7 5.7 multiply_convert_fusion
  983.4 6.4 convert_bitcast_fusion
  989.9 9.3 reshape.331
  999.1 5.7 all-to-all-start.1
  1005.6 111.1 %all-to-all-done.1 = bf16[64,75,4,128]{3,2,1,0:T(4,128)(2,1)} async-done(((bf16[64,75,4,128]{3,2,1,0:T(4,128)(2,1)}), bf16[64,75,4,128]{3,2,1,0:T(4,128)(2,1)}, u32[]{:S(2)}, u32[]{:S(2)}) %all-to-all-start.1) | async-done | bytes 4915232 | tf_op jit(solution)/shard_map/all_to_all | solution.py:148
  1116.7 7.4 copy.105
  (520 shorter events, 401.1 us)
Async XLA Ops:
  8.7 293.5 %all-to-all-start = ((bf16[1,75,256,128]{3,1,0,2:T(8,128)(2,1)}), bf16[1,75,256,128]{3,1,0,2:T(8,128)(2,1)}, u32[]{:S(2)}, u32[]{:S(2)}) async-start(bf16[1,75,256,128]{3,1,0,2:T(8,128)(2,1)} %copy.72), calls=%async_computation | async-start | bytes 10485760 | tf_op jit(solution)/shard_map/all_to_all | solution.py:107
  21.5 116.4 %collective-permute-start.2 = (bf16[75,1,128]{0,2,1:T(8,128)(2,1)S(1)}, bf16[75,1,128]{0,2,1:T(8,128)(2,1)S(1)}, u32[]{:S(2)}, u32[]{:S(2)}) collective-permute-start(bf16[75,1,128]{0,2,1:T(8,128)(2,1)S(1)} %get-tuple-element.133), channel_id=1, source_target_pairs={{4,0},{8,4},{12,8},{16,12},{20,16},{24,20},{28,24},{32,28},{36,32}... | collective-permute-start | bytes 57608 | tf_op jit(solution)/shard_map/ppermute | solution.py:26
  22.9 114.9 %collective-permute-start.1 = (bf16[75,1,128]{0,2,1:T(8,128)(2,1)S(1)}, bf16[75,1,128]{0,2,1:T(8,128)(2,1)S(1)}, u32[]{:S(2)}, u32[]{:S(2)}) collective-permute-start(bf16[75,1,128]{0,2,1:T(8,128)(2,1)S(1)} %get-tuple-element.132), channel_id=1, source_target_pairs={{0,4},{4,8},{8,12},{12,16},{16,20},{20,24},{24,28},{28,32},{32,36}... | collective-permute-start | bytes 57608 | tf_op jit(solution)/shard_map/ppermute | solution.py:25
  138.1 15.2 %collective-permute-start.6 = (bf16[75,1,128]{0,2,1:T(8,128)(2,1)S(1)}, bf16[75,1,128]{0,2,1:T(8,128)(2,1)S(1)}, u32[]{:S(2)}, u32[]{:S(2)}) collective-permute-start(bf16[75,1,128]{0,2,1:T(8,128)(2,1)S(1)} %get-tuple-element.129), channel_id=1, source_target_pairs={{4,0},{8,4},{12,8},{16,12},{20,16},{24,20},{28,24},{32,28},{36,32}... | collective-permute-start | bytes 57608 | tf_op jit(solution)/shard_map/ppermute | solution.py:26
  153.8 15.4 %collective-permute-start.10 = (bf16[75,1,64]{0,2,1:T(8,128)(2,1)S(1)}, bf16[75,1,64]{0,2,1:T(8,128)(2,1)S(1)}, u32[]{:S(2)}, u32[]{:S(2)}) collective-permute-start(bf16[75,1,64]{0,2,1:T(8,128)(2,1)S(1)} %get-tuple-element.181), channel_id=1, source_target_pairs={{4,0},{8,4},{12,8},{16,12},{20,16},{24,20},{28,24},{32,28},{36,32}... | collective-permute-start | bytes 28808 | tf_op jit(solution)/shard_map/ppermute | solution.py:26
  155.1 14.1 %collective-permute-start.9 = (bf16[75,1,64]{0,2,1:T(8,128)(2,1)S(1)}, bf16[75,1,64]{0,2,1:T(8,128)(2,1)S(1)}, u32[]{:S(2)}, u32[]{:S(2)}) collective-permute-start(bf16[75,1,64]{0,2,1:T(8,128)(2,1)S(1)} %get-tuple-element.180), channel_id=1, source_target_pairs={{0,4},{4,8},{8,12},{12,16},{16,20},{20,24},{24,28},{28,32},{32,36}... | collective-permute-start | bytes 28808 | tf_op jit(solution)/shard_map/ppermute | solution.py:25
  169.2 15.4 %collective-permute-start.14 = (bf16[75,1,64]{0,2,1:T(8,128)(2,1)S(1)}, bf16[75,1,64]{0,2,1:T(8,128)(2,1)S(1)}, u32[]{:S(2)}, u32[]{:S(2)}) collective-permute-start(bf16[75,1,64]{0,2,1:T(8,128)(2,1)S(1)} %get-tuple-element.177), channel_id=1, source_target_pairs={{4,0},{8,4},{12,8},{16,12},{20,16},{24,20},{28,24},{32,28},{36,32}... | collective-permute-start | bytes 28808 | tf_op jit(solution)/shard_map/ppermute | solution.py:26
  170.5 14.1 %collective-permute-start.13 = (bf16[75,1,64]{0,2,1:T(8,128)(2,1)S(1)}, bf16[75,1,64]{0,2,1:T(8,128)(2,1)S(1)}, u32[]{:S(2)}, u32[]{:S(2)}) collective-permute-start(bf16[75,1,64]{0,2,1:T(8,128)(2,1)S(1)} %get-tuple-element.176), channel_id=1, source_target_pairs={{0,4},{4,8},{8,12},{12,16},{16,20},{20,24},{24,28},{28,32},{32,36}... | collective-permute-start | bytes 28808 | tf_op jit(solution)/shard_map/ppermute | solution.py:25
  184.8 17.4 %collective-permute-start.16 = (f32[75,1,32]{0,2,1:T(8,128)S(1)}, f32[75,1,32]{0,2,1:T(8,128)S(1)}, u32[]{:S(2)}, u32[]{:S(2)}) collective-permute-start(f32[75,1,32]{0,2,1:T(8,128)S(1)} %multiply_bitcast_fusion.2), channel_id=1, source_target_pairs={{4,0},{8,4},{12,8},{16,12},{20,16},{24,20},{28,24},{32,28},{36,32}... | collective-permute-start | bytes 28808 | tf_op jit(solution)/shard_map/ppermute | solution.py:26
  186.1 16.1 %collective-permute-start.17 = (f32[75,1,32]{0,2,1:T(8,128)S(1)}, f32[75,1,32]{0,2,1:T(8,128)S(1)}, u32[]{:S(2)}, u32[]{:S(2)}) collective-permute-start(f32[75,1,32]{0,2,1:T(8,128)S(1)} %multiply_bitcast_fusion.2), channel_id=1, source_target_pairs={{0,4},{4,8},{8,12},{12,16},{16,20},{20,24},{24,28},{28,32},{32,36}... | collective-permute-start | bytes 28808 | tf_op jit(solution)/shard_map/ppermute | solution.py:25
  202.2 17.4 %collective-permute-start.20 = (f32[75,1,32]{0,2,1:T(8,128)S(1)}, f32[75,1,32]{0,2,1:T(8,128)S(1)}, u32[]{:S(2)}, u32[]{:S(2)}) collective-permute-start(f32[75,1,32]{0,2,1:T(8,128)S(1)} %fusion.369), channel_id=1, source_target_pairs={{4,0},{8,4},{12,8},{16,12},{20,16},{24,20},{28,24},{32,28},{36,32}... | collective-permute-start | bytes 28808 | tf_op jit(solution)/shard_map/ppermute | solution.py:26
  203.5 16.1 %collective-permute-start.21 = (f32[75,1,32]{0,2,1:T(8,128)S(1)}, f32[75,1,32]{0,2,1:T(8,128)S(1)}, u32[]{:S(2)}, u32[]{:S(2)}) collective-permute-start(f32[75,1,32]{0,2,1:T(8,128)S(1)} %fusion.369), channel_id=1, source_target_pairs={{0,4},{4,8},{8,12},{12,16},{16,20},{20,24},{24,28},{28,32},{32,36}... | collective-permute-start | bytes 28808 | tf_op jit(solution)/shard_map/ppermute | solution.py:25
  219.6 15.4 %collective-permute-start.24 = (f32[75,1,32]{0,2,1:T(8,128)S(1)}, f32[75,1,32]{0,2,1:T(8,128)S(1)}, u32[]{:S(2)}, u32[]{:S(2)}) collective-permute-start(f32[75,1,32]{0,2,1:T(8,128)S(1)} %fusion.360), channel_id=1, source_target_pairs={{4,0},{8,4},{12,8},{16,12},{20,16},{24,20},{28,24},{32,28},{36,32}... | collective-permute-start | bytes 28808 | tf_op jit(solution)/shard_map/ppermute | solution.py:26
  220.9 14.1 %collective-permute-start.25 = (f32[75,1,32]{0,2,1:T(8,128)S(1)}, f32[75,1,32]{0,2,1:T(8,128)S(1)}, u32[]{:S(2)}, u32[]{:S(2)}) collective-permute-start(f32[75,1,32]{0,2,1:T(8,128)S(1)} %fusion.360), channel_id=1, source_target_pairs={{0,4},{4,8},{8,12},{12,16},{16,20},{20,24},{24,28},{28,32},{32,36}... | collective-permute-start | bytes 28808 | tf_op jit(solution)/shard_map/ppermute | solution.py:25
  235.0 17.4 %collective-permute-start.30 = (bf16[75,1,64]{0,2,1:T(8,128)(2,1)S(1)}, bf16[75,1,64]{0,2,1:T(8,128)(2,1)S(1)}, u32[]{:S(2)}, u32[]{:S(2)}) collective-permute-start(bf16[75,1,64]{0,2,1:T(8,128)(2,1)S(1)} %get-tuple-element.173), channel_id=1, source_target_pairs={{4,0},{8,4},{12,8},{16,12},{20,16},{24,20},{28,24},{32,28},{36,32}... | collective-permute-start | bytes 28808 | tf_op jit(solution)/shard_map/ppermute | solution.py:26
  236.3 16.1 %collective-permute-start.29 = (bf16[75,1,64]{0,2,1:T(8,128)(2,1)S(1)}, bf16[75,1,64]{0,2,1:T(8,128)(2,1)S(1)}, u32[]{:S(2)}, u32[]{:S(2)}) collective-permute-start(bf16[75,1,64]{0,2,1:T(8,128)(2,1)S(1)} %get-tuple-element.172), channel_id=1, source_target_pairs={{0,4},{4,8},{8,12},{12,16},{16,20},{20,24},{24,28},{28,32},{32,36}... | collective-permute-start | bytes 28808 | tf_op jit(solution)/shard_map/ppermute | solution.py:25
  252.5 14.5 %collective-permute-start.35 = (bf16[75,2,1]{0,2,1:T(2,128)(2,1)S(1)}, bf16[75,2,1]{0,2,1:T(2,128)(2,1)S(1)}, u32[]{:S(2)}, u32[]{:S(2)}) collective-permute-start(bf16[75,2,1]{0,2,1:T(2,128)(2,1)S(1)} %get-tuple-element.171), channel_id=1, source_target_pairs={{1,0},{2,1},{3,2},{5,4},{6,5},{7,6},{9,8},{10,9},{11,10},{13,12},{... | collective-permute-start | bytes 908 | tf_op jit(solution)/shard_map/ppermute | solution.py:26
  268.0 15.5 %collective-permute-start.38 = (bf16[75,1,128]{0,2,1:T(8,128)(2,1)S(1)}, bf16[75,1,128]{0,2,1:T(8,128)(2,1)S(1)}, u32[]{:S(2)}, u32[]{:S(2)}) collective-permute-start(bf16[75,1,128]{0,2,1:T(8,128)(2,1)S(1)} %get-tuple-element.125), channel_id=1, source_target_pairs={{4,0},{8,4},{12,8},{16,12},{20,16},{24,20},{28,24},{32,28},{36,32}... | collective-permute-start | bytes 57608 | tf_op jit(solution)/shard_map/ppermute | solution.py:26
  269.3 14.2 %collective-permute-start.37 = (bf16[75,1,128]{0,2,1:T(8,128)(2,1)S(1)}, bf16[75,1,128]{0,2,1:T(8,128)(2,1)S(1)}, u32[]{:S(2)}, u32[]{:S(2)}) collective-permute-start(bf16[75,1,128]{0,2,1:T(8,128)(2,1)S(1)} %get-tuple-element.124), channel_id=1, source_target_pairs={{0,4},{4,8},{8,12},{12,16},{16,20},{20,24},{24,28},{28,32},{32,36}... | collective-permute-start | bytes 57608 | tf_op jit(solution)/shard_map/ppermute | solution.py:25
  284.4 17.0 %collective-permute-start.42 = (bf16[75,1,128]{0,2,1:T(8,128)(2,1)S(1)}, bf16[75,1,128]{0,2,1:T(8,128)(2,1)S(1)}, u32[]{:S(2)}, u32[]{:S(2)}) collective-permute-start(bf16[75,1,128]{0,2,1:T(8,128)(2,1)S(1)} %get-tuple-element.121), channel_id=1, source_target_pairs={{4,0},{8,4},{12,8},{16,12},{20,16},{24,20},{28,24},{32,28},{36,32}... | collective-permute-start | bytes 57608 | tf_op jit(solution)/shard_map/ppermute | solution.py:26
  285.7 15.7 %collective-permute-start.41 = (bf16[75,1,128]{0,2,1:T(8,128)(2,1)S(1)}, bf16[75,1,128]{0,2,1:T(8,128)(2,1)S(1)}, u32[]{:S(2)}, u32[]{:S(2)}) collective-permute-start(bf16[75,1,128]{0,2,1:T(8,128)(2,1)S(1)} %get-tuple-element.120), channel_id=1, source_target_pairs={{0,4},{4,8},{8,12},{12,16},{16,20},{20,24},{24,28},{28,32},{32,36}... | collective-permute-start | bytes 57608 | tf_op jit(solution)/shard_map/ppermute | solution.py:25
  421.2 16.7 %collective-permute-start.46 = (bf16[75,1,128]{0,2,1:T(8,128)(2,1)S(1)}, bf16[75,1,128]{0,2,1:T(8,128)(2,1)S(1)}, u32[]{:S(2)}, u32[]{:S(2)}) collective-permute-start(bf16[75,1,128]{0,2,1:T(8,128)(2,1)S(1)} %get-tuple-element.117), channel_id=1, source_target_pairs={{4,0},{8,4},{12,8},{16,12},{20,16},{24,20},{28,24},{32,28},{36,32}... | collective-permute-start | bytes 57608 | tf_op jit(solution)/shard_map/ppermute | solution.py:26
  422.5 15.4 %collective-permute-start.45 = (bf16[75,1,128]{0,2,1:T(8,128)(2,1)S(1)}, bf16[75,1,128]{0,2,1:T(8,128)(2,1)S(1)}, u32[]{:S(2)}, u32[]{:S(2)}) collective-permute-start(bf16[75,1,128]{0,2,1:T(8,128)(2,1)S(1)} %get-tuple-element.116), channel_id=1, source_target_pairs={{0,4},{4,8},{8,12},{12,16},{16,20},{20,24},{24,28},{28,32},{32,36}... | collective-permute-start | bytes 57608 | tf_op jit(solution)/shard_map/ppermute | solution.py:25
  438.1 14.2 %collective-permute-start.50 = (bf16[75,1,128]{0,2,1:T(8,128)(2,1)S(1)}, bf16[75,1,128]{0,2,1:T(8,128)(2,1)S(1)}, u32[]{:S(2)}, u32[]{:S(2)}) collective-permute-start(bf16[75,1,128]{0,2,1:T(8,128)(2,1)S(1)} %get-tuple-element.113), channel_id=1, source_target_pairs={{4,0},{8,4},{12,8},{16,12},{20,16},{24,20},{28,24},{32,28},{36,32}... | collective-permute-start | bytes 57608 | tf_op jit(solution)/shard_map/ppermute | solution.py:26
  452.8 14.2 %collective-permute-start.54 = (bf16[75,1,64]{0,2,1:T(8,128)(2,1)S(1)}, bf16[75,1,64]{0,2,1:T(8,128)(2,1)S(1)}, u32[]{:S(2)}, u32[]{:S(2)}) collective-permute-start(bf16[75,1,64]{0,2,1:T(8,128)(2,1)S(1)} %get-tuple-element.165), channel_id=1, source_target_pairs={{4,0},{8,4},{12,8},{16,12},{20,16},{24,20},{28,24},{32,28},{36,32}... | collective-permute-start | bytes 28808 | tf_op jit(solution)/shard_map/ppermute | solution.py:26
  467.0 14.2 %collective-permute-start.58 = (bf16[75,1,64]{0,2,1:T(8,128)(2,1)S(1)}, bf16[75,1,64]{0,2,1:T(8,128)(2,1)S(1)}, u32[]{:S(2)}, u32[]{:S(2)}) collective-permute-start(bf16[75,1,64]{0,2,1:T(8,128)(2,1)S(1)} %get-tuple-element.161), channel_id=1, source_target_pairs={{4,0},{8,4},{12,8},{16,12},{20,16},{24,20},{28,24},{32,28},{36,32}... | collective-permute-start | bytes 28808 | tf_op jit(solution)/shard_map/ppermute | solution.py:26
  481.4 16.9 %collective-permute-start.60 = (f32[75,1,32]{0,2,1:T(8,128)S(1)}, f32[75,1,32]{0,2,1:T(8,128)S(1)}, u32[]{:S(2)}, u32[]{:S(2)}) collective-permute-start(f32[75,1,32]{0,2,1:T(8,128)S(1)} %multiply_bitcast_fusion.1), channel_id=1, source_target_pairs={{4,0},{8,4},{12,8},{16,12},{20,16},{24,20},{28,24},{32,28},{36,32}... | collective-permute-start | bytes 28808 | tf_op jit(solution)/shard_map/ppermute | solution.py:26
  482.6 15.6 %collective-permute-start.61 = (f32[75,1,32]{0,2,1:T(8,128)S(1)}, f32[75,1,32]{0,2,1:T(8,128)S(1)}, u32[]{:S(2)}, u32[]{:S(2)}) collective-permute-start(f32[75,1,32]{0,2,1:T(8,128)S(1)} %multiply_bitcast_fusion.1), channel_id=1, source_target_pairs={{0,4},{4,8},{8,12},{12,16},{16,20},{20,24},{24,28},{28,32},{32,36}... | collective-permute-start | bytes 28808 | tf_op jit(solution)/shard_map/ppermute | solution.py:25
  498.3 17.4 %collective-permute-start.64 = (f32[75,1,32]{0,2,1:T(8,128)S(1)}, f32[75,1,32]{0,2,1:T(8,128)S(1)}, u32[]{:S(2)}, u32[]{:S(2)}) collective-permute-start(f32[75,1,32]{0,2,1:T(8,128)S(1)} %fusion.341), channel_id=1, source_target_pairs={{4,0},{8,4},{12,8},{16,12},{20,16},{24,20},{28,24},{32,28},{36,32}... | collective-permute-start | bytes 28808 | tf_op jit(solution)/shard_map/ppermute | solution.py:26
  499.6 16.1 %collective-permute-start.65 = (f32[75,1,32]{0,2,1:T(8,128)S(1)}, f32[75,1,32]{0,2,1:T(8,128)S(1)}, u32[]{:S(2)}, u32[]{:S(2)}) collective-permute-start(f32[75,1,32]{0,2,1:T(8,128)S(1)} %fusion.341), channel_id=1, source_target_pairs={{0,4},{4,8},{8,12},{12,16},{16,20},{20,24},{24,28},{28,32},{32,36}... | collective-permute-start | bytes 28808 | tf_op jit(solution)/shard_map/ppermute | solution.py:25
  515.7 15.4 %collective-permute-start.68 = (f32[75,1,32]{0,2,1:T(8,128)S(1)}, f32[75,1,32]{0,2,1:T(8,128)S(1)}, u32[]{:S(2)}, u32[]{:S(2)}) collective-permute-start(f32[75,1,32]{0,2,1:T(8,128)S(1)} %fusion.332), channel_id=1, source_target_pairs={{4,0},{8,4},{12,8},{16,12},{20,16},{24,20},{28,24},{32,28},{36,32}... | collective-permute-start | bytes 28808 | tf_op jit(solution)/shard_map/ppermute | solution.py:26
  517.0 14.1 %collective-permute-start.69 = (f32[75,1,32]{0,2,1:T(8,128)S(1)}, f32[75,1,32]{0,2,1:T(8,128)S(1)}, u32[]{:S(2)}, u32[]{:S(2)}) collective-permute-start(f32[75,1,32]{0,2,1:T(8,128)S(1)} %fusion.332), channel_id=1, source_target_pairs={{0,4},{4,8},{8,12},{12,16},{16,20},{20,24},{24,28},{28,32},{32,36}... | collective-permute-start | bytes 28808 | tf_op jit(solution)/shard_map/ppermute | solution.py:25
  531.1 17.5 %collective-permute-start.74 = (bf16[75,1,64]{0,2,1:T(8,128)(2,1)S(1)}, bf16[75,1,64]{0,2,1:T(8,128)(2,1)S(1)}, u32[]{:S(2)}, u32[]{:S(2)}) collective-permute-start(bf16[75,1,64]{0,2,1:T(8,128)(2,1)S(1)} %get-tuple-element.157), channel_id=1, source_target_pairs={{4,0},{8,4},{12,8},{16,12},{20,16},{24,20},{28,24},{32,28},{36,32}... | collective-permute-start | bytes 28808 | tf_op jit(solution)/shard_map/ppermute | solution.py:26
  532.4 16.2 %collective-permute-start.73 = (bf16[75,1,64]{0,2,1:T(8,128)(2,1)S(1)}, bf16[75,1,64]{0,2,1:T(8,128)(2,1)S(1)}, u32[]{:S(2)}, u32[]{:S(2)}) collective-permute-start(bf16[75,1,64]{0,2,1:T(8,128)(2,1)S(1)} %get-tuple-element.156), channel_id=1, source_target_pairs={{0,4},{4,8},{8,12},{12,16},{16,20},{20,24},{24,28},{28,32},{32,36}... | collective-permute-start | bytes 28808 | tf_op jit(solution)/shard_map/ppermute | solution.py:25
  548.7 16.3 %collective-permute-start.78 = (bf16[75,1,64]{0,2,1:T(8,128)(2,1)S(1)}, bf16[75,1,64]{0,2,1:T(8,128)(2,1)S(1)}, u32[]{:S(2)}, u32[]{:S(2)}) collective-permute-start(bf16[75,1,64]{0,2,1:T(8,128)(2,1)S(1)} %get-tuple-element.153), channel_id=1, source_target_pairs={{4,0},{8,4},{12,8},{16,12},{20,16},{24,20},{28,24},{32,28},{36,32}... | collective-permute-start | bytes 28808 | tf_op jit(solution)/shard_map/ppermute | solution.py:26
  550.0 15.0 %collective-permute-start.77 = (bf16[75,1,64]{0,2,1:T(8,128)(2,1)S(1)}, bf16[75,1,64]{0,2,1:T(8,128)(2,1)S(1)}, u32[]{:S(2)}, u32[]{:S(2)}) collective-permute-start(bf16[75,1,64]{0,2,1:T(8,128)(2,1)S(1)} %get-tuple-element.152), channel_id=1, source_target_pairs={{0,4},{4,8},{8,12},{12,16},{16,20},{20,24},{24,28},{28,32},{32,36}... | collective-permute-start | bytes 28808 | tf_op jit(solution)/shard_map/ppermute | solution.py:25
  567.2 21.2 %collective-permute-start.83 = (bf16[75,4,1]{0,2,1:T(2,128)(2,1)}, bf16[75,4,1]{0,2,1:T(2,128)(2,1)S(1)}, u32[]{:S(2)}, u32[]{:S(2)}) collective-permute-start(bf16[75,4,1]{0,2,1:T(2,128)(2,1)} %get-tuple-element.111), channel_id=1, source_target_pairs={{1,0},{2,1},{3,2},{5,4},{6,5},{7,6},{9,8},{10,9},{11,10},{13,12},{... | collective-permute-start | bytes 1808 | tf_op jit(solution)/shard_map/ppermute | solution.py:26
  569.1 19.3 %collective-permute-start.80 = (bf16[75,4,1]{0,2,1:T(2,128)(2,1)}, bf16[75,4,1]{0,2,1:T(2,128)(2,1)}, u32[]{:S(2)}, u32[]{:S(2)}) collective-permute-start(bf16[75,4,1]{0,2,1:T(2,128)(2,1)} %get-tuple-element.110), channel_id=1, source_target_pairs={{0,1},{1,2},{2,3},{4,5},{5,6},{6,7},{8,9},{9,10},{10,11},{12,13},{... | collective-permute-start | bytes 1808 | tf_op jit(solution)/shard_map/ppermute | solution.py:25
  573.0 15.4 %collective-permute-start.82 = (bf16[75,1,128]{0,2,1:T(8,128)(2,1)}, bf16[75,1,128]{0,2,1:T(8,128)(2,1)S(1)}, u32[]{:S(2)}, u32[]{:S(2)}) collective-permute-start(bf16[75,1,128]{0,2,1:T(8,128)(2,1)} %get-tuple-element.109), channel_id=1, source_target_pairs={{4,0},{8,4},{12,8},{16,12},{20,16},{24,20},{28,24},{32,28},{36,32}... | collective-permute-start | bytes 57608 | tf_op jit(solution)/shard_map/ppermute | solution.py:26
  592.2 25.4 %collective-permute-start.87 = (bf16[75,4,1]{0,2,1:T(2,128)(2,1)}, bf16[75,4,1]{0,2,1:T(2,128)(2,1)S(1)}, u32[]{:S(2)}, u32[]{:S(2)}) collective-permute-start(bf16[75,4,1]{0,2,1:T(2,128)(2,1)} %get-tuple-element.107), channel_id=1, source_target_pairs={{1,0},{2,1},{3,2},{5,4},{6,5},{7,6},{9,8},{10,9},{11,10},{13,12},{... | collective-permute-start | bytes 1808 | tf_op jit(solution)/shard_map/ppermute | solution.py:26
  594.7 23.0 %collective-permute-start.84 = (bf16[75,4,1]{0,2,1:T(2,128)(2,1)}, bf16[75,4,1]{0,2,1:T(2,128)(2,1)}, u32[]{:S(2)}, u32[]{:S(2)}) collective-permute-start(bf16[75,4,1]{0,2,1:T(2,128)(2,1)} %get-tuple-element.106), channel_id=1, source_target_pairs={{0,1},{1,2},{2,3},{4,5},{5,6},{6,7},{8,9},{9,10},{10,11},{12,13},{... | collective-permute-start | bytes 1808 | tf_op jit(solution)/shard_map/ppermute | solution.py:25
  598.1 19.6 %collective-permute-start.86 = (bf16[75,1,128]{0,2,1:T(8,128)(2,1)}, bf16[75,1,128]{0,2,1:T(8,128)(2,1)S(1)}, u32[]{:S(2)}, u32[]{:S(2)}) collective-permute-start(bf16[75,1,128]{0,2,1:T(8,128)(2,1)} %get-tuple-element.105), channel_id=1, source_target_pairs={{4,0},{8,4},{12,8},{16,12},{20,16},{24,20},{28,24},{32,28},{36,32}... | collective-permute-start | bytes 57608 | tf_op jit(solution)/shard_map/ppermute | solution.py:26
  599.4 18.3 %collective-permute-start.85 = (bf16[75,1,128]{0,2,1:T(8,128)(2,1)}, bf16[75,1,128]{0,2,1:T(8,128)(2,1)}, u32[]{:S(2)}, u32[]{:S(2)}) collective-permute-start(bf16[75,1,128]{0,2,1:T(8,128)(2,1)} %get-tuple-element.104), channel_id=1, source_target_pairs={{0,4},{4,8},{8,12},{12,16},{16,20},{20,24},{24,28},{28,32},{32,36}... | collective-permute-start | bytes 57608 | tf_op jit(solution)/shard_map/ppermute | solution.py:25
  700.4 14.8 %collective-permute-start.90 = (bf16[75,1,128]{0,2,1:T(8,128)(2,1)S(1)}, bf16[75,1,128]{0,2,1:T(8,128)(2,1)S(1)}, u32[]{:S(2)}, u32[]{:S(2)}) collective-permute-start(bf16[75,1,128]{0,2,1:T(8,128)(2,1)S(1)} %get-tuple-element.101), channel_id=1, source_target_pairs={{4,0},{8,4},{12,8},{16,12},{20,16},{24,20},{28,24},{32,28},{36,32}... | collective-permute-start | bytes 57608 | tf_op jit(solution)/shard_map/ppermute | solution.py:26
  715.4 14.2 %collective-permute-start.94 = (bf16[75,1,128]{0,2,1:T(8,128)(2,1)S(1)}, bf16[75,1,128]{0,2,1:T(8,128)(2,1)S(1)}, u32[]{:S(2)}, u32[]{:S(2)}) collective-permute-start(bf16[75,1,128]{0,2,1:T(8,128)(2,1)S(1)} %get-tuple-element.97), channel_id=1, source_target_pairs={{4,0},{8,4},{12,8},{16,12},{20,16},{24,20},{28,24},{32,28},{36,32}... | collective-permute-start | bytes 57608 | tf_op jit(solution)/shard_map/ppermute | solution.py:26
  730.1 14.2 %collective-permute-start.98 = (bf16[75,1,64]{0,2,1:T(8,128)(2,1)S(1)}, bf16[75,1,64]{0,2,1:T(8,128)(2,1)S(1)}, u32[]{:S(2)}, u32[]{:S(2)}) collective-permute-start(bf16[75,1,64]{0,2,1:T(8,128)(2,1)S(1)} %get-tuple-element.149), channel_id=1, source_target_pairs={{4,0},{8,4},{12,8},{16,12},{20,16},{24,20},{28,24},{32,28},{36,32}... | collective-permute-start | bytes 28808 | tf_op jit(solution)/shard_map/ppermute | solution.py:26
  744.3 14.2 %collective-permute-start.102 = (bf16[75,1,64]{0,2,1:T(8,128)(2,1)S(1)}, bf16[75,1,64]{0,2,1:T(8,128)(2,1)S(1)}, u32[]{:S(2)}, u32[]{:S(2)}) collective-permute-start(bf16[75,1,64]{0,2,1:T(8,128)(2,1)S(1)} %get-tuple-element.145), channel_id=1, source_target_pairs={{4,0},{8,4},{12,8},{16,12},{20,16},{24,20},{28,24},{32,28},{36,32}... | collective-permute-start | bytes 28808 | tf_op jit(solution)/shard_map/ppermute | solution.py:26
  758.7 16.9 %collective-permute-start.104 = (f32[75,1,32]{0,2,1:T(8,128)S(1)}, f32[75,1,32]{0,2,1:T(8,128)S(1)}, u32[]{:S(2)}, u32[]{:S(2)}) collective-permute-start(f32[75,1,32]{0,2,1:T(8,128)S(1)} %multiply_bitcast_fusion), channel_id=1, source_target_pairs={{4,0},{8,4},{12,8},{16,12},{20,16},{24,20},{28,24},{32,28},{36,32}... | collective-permute-start | bytes 28808 | tf_op jit(solution)/shard_map/ppermute | solution.py:26
  760.0 15.6 %collective-permute-start.105 = (f32[75,1,32]{0,2,1:T(8,128)S(1)}, f32[75,1,32]{0,2,1:T(8,128)S(1)}, u32[]{:S(2)}, u32[]{:S(2)}) collective-permute-start(f32[75,1,32]{0,2,1:T(8,128)S(1)} %multiply_bitcast_fusion), channel_id=1, source_target_pairs={{0,4},{4,8},{8,12},{12,16},{16,20},{20,24},{24,28},{28,32},{32,36}... | collective-permute-start | bytes 28808 | tf_op jit(solution)/shard_map/ppermute | solution.py:25
  775.6 17.4 %collective-permute-start.108 = (f32[75,1,32]{0,2,1:T(8,128)S(1)}, f32[75,1,32]{0,2,1:T(8,128)S(1)}, u32[]{:S(2)}, u32[]{:S(2)}) collective-permute-start(f32[75,1,32]{0,2,1:T(8,128)S(1)} %fusion.313), channel_id=1, source_target_pairs={{4,0},{8,4},{12,8},{16,12},{20,16},{24,20},{28,24},{32,28},{36,32}... | collective-permute-start | bytes 28808 | tf_op jit(solution)/shard_map/ppermute | solution.py:26
  776.9 16.1 %collective-permute-start.109 = (f32[75,1,32]{0,2,1:T(8,128)S(1)}, f32[75,1,32]{0,2,1:T(8,128)S(1)}, u32[]{:S(2)}, u32[]{:S(2)}) collective-permute-start(f32[75,1,32]{0,2,1:T(8,128)S(1)} %fusion.313), channel_id=1, source_target_pairs={{0,4},{4,8},{8,12},{12,16},{16,20},{20,24},{24,28},{28,32},{32,36}... | collective-permute-start | bytes 28808 | tf_op jit(solution)/shard_map/ppermute | solution.py:25
  793.0 15.4 %collective-permute-start.112 = (f32[75,1,32]{0,2,1:T(8,128)S(1)}, f32[75,1,32]{0,2,1:T(8,128)S(1)}, u32[]{:S(2)}, u32[]{:S(2)}) collective-permute-start(f32[75,1,32]{0,2,1:T(8,128)S(1)} %fusion.304), channel_id=1, source_target_pairs={{4,0},{8,4},{12,8},{16,12},{20,16},{24,20},{28,24},{32,28},{36,32}... | collective-permute-start | bytes 28808 | tf_op jit(solution)/shard_map/ppermute | solution.py:26
  808.5 17.5 %collective-permute-start.118 = (bf16[75,1,64]{0,2,1:T(8,128)(2,1)S(1)}, bf16[75,1,64]{0,2,1:T(8,128)(2,1)S(1)}, u32[]{:S(2)}, u32[]{:S(2)}) collective-permute-start(bf16[75,1,64]{0,2,1:T(8,128)(2,1)S(1)} %get-tuple-element.141), channel_id=1, source_target_pairs={{4,0},{8,4},{12,8},{16,12},{20,16},{24,20},{28,24},{32,28},{36,32}... | collective-permute-start | bytes 28808 | tf_op jit(solution)/shard_map/ppermute | solution.py:26
  809.8 16.2 %collective-permute-start.117 = (bf16[75,1,64]{0,2,1:T(8,128)(2,1)S(1)}, bf16[75,1,64]{0,2,1:T(8,128)(2,1)S(1)}, u32[]{:S(2)}, u32[]{:S(2)}) collective-permute-start(bf16[75,1,64]{0,2,1:T(8,128)(2,1)S(1)} %get-tuple-element.140), channel_id=1, source_target_pairs={{0,4},{4,8},{8,12},{12,16},{16,20},{20,24},{24,28},{28,32},{32,36}... | collective-permute-start | bytes 28808 | tf_op jit(solution)/shard_map/ppermute | solution.py:25
  826.1 16.3 %collective-permute-start.122 = (bf16[75,1,64]{0,2,1:T(8,128)(2,1)S(1)}, bf16[75,1,64]{0,2,1:T(8,128)(2,1)S(1)}, u32[]{:S(2)}, u32[]{:S(2)}) collective-permute-start(bf16[75,1,64]{0,2,1:T(8,128)(2,1)S(1)} %get-tuple-element.137), channel_id=1, source_target_pairs={{4,0},{8,4},{12,8},{16,12},{20,16},{24,20},{28,24},{32,28},{36,32}... | collective-permute-start | bytes 28808 | tf_op jit(solution)/shard_map/ppermute | solution.py:26
  827.4 15.0 %collective-permute-start.121 = (bf16[75,1,64]{0,2,1:T(8,128)(2,1)S(1)}, bf16[75,1,64]{0,2,1:T(8,128)(2,1)S(1)}, u32[]{:S(2)}, u32[]{:S(2)}) collective-permute-start(bf16[75,1,64]{0,2,1:T(8,128)(2,1)S(1)} %get-tuple-element.136), channel_id=1, source_target_pairs={{0,4},{4,8},{8,12},{12,16},{16,20},{20,24},{24,28},{28,32},{32,36}... | collective-permute-start | bytes 28808 | tf_op jit(solution)/shard_map/ppermute | solution.py:25
  844.5 21.2 %collective-permute-start.127 = (bf16[75,4,1]{0,2,1:T(2,128)(2,1)}, bf16[75,4,1]{0,2,1:T(2,128)(2,1)S(1)}, u32[]{:S(2)}, u32[]{:S(2)}) collective-permute-start(bf16[75,4,1]{0,2,1:T(2,128)(2,1)} %get-tuple-element.95), channel_id=1, source_target_pairs={{1,0},{2,1},{3,2},{5,4},{6,5},{7,6},{9,8},{10,9},{11,10},{13,12},{... | collective-permute-start | bytes 1808 | tf_op jit(solution)/shard_map/ppermute | solution.py:26
  846.4 19.3 %collective-permute-start.124 = (bf16[75,4,1]{0,2,1:T(2,128)(2,1)}, bf16[75,4,1]{0,2,1:T(2,128)(2,1)}, u32[]{:S(2)}, u32[]{:S(2)}) collective-permute-start(bf16[75,4,1]{0,2,1:T(2,128)(2,1)} %get-tuple-element.94), channel_id=1, source_target_pairs={{0,1},{1,2},{2,3},{4,5},{5,6},{6,7},{8,9},{9,10},{10,11},{12,13},{... | collective-permute-start | bytes 1808 | tf_op jit(solution)/shard_map/ppermute | solution.py:25
  850.3 15.3 %collective-permute-start.126 = (bf16[75,1,128]{0,2,1:T(8,128)(2,1)}, bf16[75,1,128]{0,2,1:T(8,128)(2,1)S(1)}, u32[]{:S(2)}, u32[]{:S(2)}) collective-permute-start(bf16[75,1,128]{0,2,1:T(8,128)(2,1)} %get-tuple-element.93), channel_id=1, source_target_pairs={{4,0},{8,4},{12,8},{16,12},{20,16},{24,20},{28,24},{32,28},{36,32}... | collective-permute-start | bytes 57608 | tf_op jit(solution)/shard_map/ppermute | solution.py:26
  869.5 25.6 %collective-permute-start.131 = (bf16[75,4,1]{0,2,1:T(2,128)(2,1)}, bf16[75,4,1]{0,2,1:T(2,128)(2,1)S(1)}, u32[]{:S(2)}, u32[]{:S(2)}) collective-permute-start(bf16[75,4,1]{0,2,1:T(2,128)(2,1)} %get-tuple-element.91), channel_id=1, source_target_pairs={{1,0},{2,1},{3,2},{5,4},{6,5},{7,6},{9,8},{10,9},{11,10},{13,12},{... | collective-permute-start | bytes 1808 | tf_op jit(solution)/shard_map/ppermute | solution.py:26
  872.0 23.1 %collective-permute-start.128 = (bf16[75,4,1]{0,2,1:T(2,128)(2,1)}, bf16[75,4,1]{0,2,1:T(2,128)(2,1)}, u32[]{:S(2)}, u32[]{:S(2)}) collective-permute-start(bf16[75,4,1]{0,2,1:T(2,128)(2,1)} %get-tuple-element.90), channel_id=1, source_target_pairs={{0,1},{1,2},{2,3},{4,5},{5,6},{6,7},{8,9},{9,10},{10,11},{12,13},{... | collective-permute-start | bytes 1808 | tf_op jit(solution)/shard_map/ppermute | solution.py:25
  875.4 19.8 %collective-permute-start.130 = (bf16[75,1,128]{0,2,1:T(8,128)(2,1)}, bf16[75,1,128]{0,2,1:T(8,128)(2,1)S(1)}, u32[]{:S(2)}, u32[]{:S(2)}) collective-permute-start(bf16[75,1,128]{0,2,1:T(8,128)(2,1)} %get-tuple-element.89), channel_id=1, source_target_pairs={{4,0},{8,4},{12,8},{16,12},{20,16},{24,20},{28,24},{32,28},{36,32}... | collective-permute-start | bytes 57608 | tf_op jit(solution)/shard_map/ppermute | solution.py:26
  876.7 18.5 %collective-permute-start.129 = (bf16[75,1,128]{0,2,1:T(8,128)(2,1)}, bf16[75,1,128]{0,2,1:T(8,128)(2,1)}, u32[]{:S(2)}, u32[]{:S(2)}) collective-permute-start(bf16[75,1,128]{0,2,1:T(8,128)(2,1)} %get-tuple-element.88), channel_id=1, source_target_pairs={{0,4},{4,8},{8,12},{12,16},{16,20},{20,24},{24,28},{28,32},{32,36}... | collective-permute-start | bytes 57608 | tf_op jit(solution)/shard_map/ppermute | solution.py:25
  999.1 117.5 %all-to-all-start.1 = ((bf16[64,75,4,128]{3,2,1,0:T(4,128)(2,1)}), bf16[64,75,4,128]{3,2,1,0:T(4,128)(2,1)}, u32[]{:S(2)}, u32[]{:S(2)}) async-start(bf16[64,75,4,128]{3,2,1,0:T(4,128)(2,1)} %reshape.331), calls=%async_computation.1 | async-start | bytes 9830400 | tf_op jit(solution)/shard_map/all_to_all | solution.py:148
  (88 other events, 1737.2 us)
